TPU v7x, 128 devices: a whole 4x4x4 slice. The times are simulated.
128 devices in a mesh: ctx: 8 (over z_lo, y), tp: 16 (over z_hi, x, core).
Axes of the slice: x: 4, y: 4, z: 4 (z_hi: 2, z_lo: 2; z = z_hi * 2 + z_lo), core: 2. Of those that a mesh axis runs over, the one named last changes fastest.
Arguments:
- queries: bfloat16 [8192, 8192], P('ctx', 'tp'), may hold values from -64 to 64
- context_keys: bfloat16 [8192, 1024], P('ctx'), may hold values from -6 to 6
- context_values: bfloat16 [8192, 1024], P('ctx'), may hold values from -6 to 6
- positions: int32 [8192], P('ctx'), may hold values from 0 to 8191, as said below
- out_weight: bfloat16 [8192, 8192], P('tp'), may hold values from -0.5 to 0.5
- residual_in: bfloat16 [8192, 8192], P(('ctx', 'tp')), may hold values from -3 to 3
- norm_gain: float32 [8192], replicated, may hold values from 0.5 to 1.5
- static_scale: float32 [1], replicated, may hold values from 0.004 to 0.009
Outputs:
- hidden_out: bfloat16 [8192, 8192], P(('ctx', 'tp'))
- clipped: bfloat16 [8192, 8192], P(('ctx', 'tp'))
Inputs may be any that keep to these rules, and one draw needn't show every extreme that they name: Rows fall into aligned runs of 512 rows that hold consecutive positions in increasing order; all positions together are a permutation of 0 to 8191.
All inputs are finite; a program needn't handle non-finite values.
Results may differ from a plain program's by a relative error of at most 0.017.
Values may be sent and summed in bfloat16 or wider, within the bound.
A program may use at most 128 MiB of HBM per device.

v0:
```python
import math

import jax
import jax.numpy as jnp
from jax import lax
from jax.sharding import PartitionSpec as P

KVH = 8
HD = 128


masked_fill = -1e30


def sent_to_all(array, axis):
    count = lax.axis_size(axis)
    return lax.all_to_all(
        jnp.broadcast_to(array[None], (count, *array.shape)), axis, 0, 0, tiled=True
    )


def joined_along(pieces, dim):
    shape = list(pieces.shape[1:])
    shape[dim] *= pieces.shape[0]
    return jnp.moveaxis(pieces, 0, dim).reshape(shape)


def gathered_copies(array, axis, dim):
    pieces = sent_to_all(array, axis)
    return joined_along(pieces, dim)


def shifted(value, axis, steps):
    count = lax.axis_size(axis)
    pairs = [(source, (source + steps) % count) for source in range(count)]
    return lax.ppermute(value, axis, pairs)


def update_block(carry, query_blk, query_pos, key_blk, value_blk, key_pos):
    run_max, run_total, accum = carry
    scores = jnp.einsum("qhd,kd->hqk", query_blk, key_blk, preferred_element_type=jnp.float32) * (
        1.0 / math.sqrt(query_blk.shape[2])
    )
    allowed = key_pos[None, None, :] <= query_pos[None, :, None]
    new_max = jnp.maximum(run_max, jnp.max(jnp.where(allowed, scores, masked_fill), axis=2))
    expo = jnp.where(allowed, jnp.exp(scores - new_max[:, :, None]), 0.0)
    factor = jnp.exp(run_max - new_max)
    run_total = run_total * factor + jnp.sum(expo, axis=2)
    weights = expo.astype(jnp.bfloat16)
    accum = accum * factor[:, :, None] + jnp.einsum(
        "hqk,kd->hqd", weights, value_blk, preferred_element_type=jnp.float32
    )
    return (new_max, run_total, accum)


def attend_keys(carry, query_heads, query_pos, key_blk, value_blk, key_pos):
    return update_block(carry, query_heads, query_pos, key_blk, value_blk, key_pos)


def shards(
    queries,
    context_keys,
    context_values,
    positions,
    out_weight,
    residual_in,
    norm_gain,
    static_scale,
):
    ctx_count = lax.axis_size("ctx")
    tp_count = lax.axis_size("tp")
    ctx_rank = lax.axis_index("ctx")
    tp_rank = lax.axis_index("tp")
    tok_rows = queries.shape[0]
    head_count = queries.shape[1] // HD
    share_count = tp_count // KVH
    kv_group = tp_rank // share_count
    own_keys = lax.dynamic_slice_in_dim(context_keys, kv_group * HD, HD, 1)
    own_values = lax.dynamic_slice_in_dim(context_values, kv_group * HD, HD, 1)
    every_pos = gathered_copies(positions, "ctx", 0)
    query_heads = queries.reshape(tok_rows, head_count, HD)
    carry = (
        jnp.full((head_count, tok_rows), masked_fill, jnp.float32),
        jnp.zeros((head_count, tok_rows), jnp.float32),
        jnp.zeros((head_count, tok_rows, HD), jnp.float32),
    )
    carry = attend_keys(carry, query_heads, positions, own_keys, own_values, positions)

    def source_pos(cycle_step):
        source = (ctx_rank - cycle_step) % ctx_count
        return lax.dynamic_slice_in_dim(every_pos, source * tok_rows, tok_rows, 0)

    def cycle_turn(cycle_step, loop_carry):
        key_buf, value_buf, inner_carry = loop_carry
        key_buf, value_buf = shifted((key_buf, value_buf), "ctx", 1)
        inner_carry = attend_keys(
            inner_carry, query_heads, positions, key_buf, value_buf, source_pos(cycle_step)
        )
        return (key_buf, value_buf, inner_carry)

    finished = lax.fori_loop(1, ctx_count, cycle_turn, (own_keys, own_values, carry))
    run_max, run_total, accum = finished[2]
    attended = (accum / run_total[:, :, None]).astype(jnp.bfloat16)
    attended = jnp.transpose(attended, (1, 0, 2)).reshape(tok_rows, head_count * HD)
    mine = lax.psum_scatter(
        jnp.dot(attended, out_weight, preferred_element_type=jnp.float32).astype(jnp.bfloat16),
        "tp",
        scatter_dimension=0,
        tiled=True,
    ).astype(jnp.float32)
    summed = residual_in.astype(jnp.float32) + mine
    hidden_out = summed.astype(jnp.bfloat16)
    inv_rms = lax.rsqrt(jnp.mean(summed * summed, axis=1, keepdims=True) + 1e-05)
    limit = 448.0 * static_scale[0]
    clipped = jnp.clip(summed * inv_rms * norm_gain[None, :], -limit, limit).astype(jnp.bfloat16)
    return (hidden_out, clipped)


def solution(mesh):
    return jax.shard_map(
        shards,
        mesh=mesh,
        in_specs=(
            P("ctx", "tp"),
            P("ctx", None),
            P("ctx", None),
            P("ctx"),
            P("tp", None),
            P(("ctx", "tp"), None),
            P(),
            P(),
        ),
        out_specs=(P(("ctx", "tp"), None), P(("ctx", "tp"), None)),
        check_vma=False,
    )
```

profile of v0, /device:TPU:1, one launch (start us, length us, event | category | flops | bytes accessed | tf_op | source)
XLA Modules:
  0.0 372.8 jit_solution(1364957910899659719)
XLA Ops:
  8.5 6.4 %all-to-all-start = ((s32[8,1,1024]{2,1,0:T(1,128)}), s32[8,1,1024]{2,1,0:T(1,128)S(1)}, u32[]{:S(2)}, u32[]{:S(2)}) async-start(s32[8,1,1024]{2,1,0:T(1,128)} %broadcast_in_dim.97), calls=%async_computation | async-start | bytes 65536 | tf_op jit(solution)/shard_map/all_to_all | solution.py:17
  25.9 5.9 %fusion.24 = f32[4,1024,128]{2,1,0:T(8,128)} fusion(f32[1024,1024,4]{1,0,2:T(8,128)S(1)} %get-tuple-element.287, f32[4,1024]{1,0:T(4,128)S(1)} %broadcast_maximum_fusion, pred[1024,1024]{0,1:T(8,128)(4,1)S(1)} %broadcast_compare_fusion.1, f32[4,1024]{1,0:T(4,128)S(1)} %get-tuple-element.284, bf16[1024,128]{1,0:T(8,128)(2,1)S(1)} %get-tuple-element.361), kind=kOutput, calls=%fused_computation.34 | convolution fusion | flops 1091043328 | bytes 20217856 | tf_op jit(solution)/shard_map/hqk,kd->hqd/dot_general | solution.py:50
  32.5 152.5 %while.23 = (s32[]{:T(128)}, bf16[1024,128]{1,0:T(8,128)(2,1)S(1)}, bf16[1024,128]{1,0:T(8,128)(2,1)S(1)}, f32[4,1024]{1,0:T(4,128)S(1)}, f32[4,1024]{1,0:T(4,12...) while((s32[]{:T(128)}, bf16[1024,128]{1,0:T(8,128)(2,1)S(1)}, ...), condition=%wide.region_5.6_spmd, body=%wide.region_2.5_spmd.sunk | while | flops 2195726336 | bytes 80495040 | solution.py:101
  35.8 5.8 %collective-permute-done = bf16[1024,128]{1,0:T(8,128)(2,1)S(1)} collective-permute-done((bf16[1024,128]{1,0:T(8,128)(2,1)S(1)}, bf16[1024,128]{1,0:T(8,128)(2,1)S(1)}, u32[]{:S(2)}, u32[]{:S(2)}) %collective-permute-start) | collective-permute-done | bytes 262176 | tf_op jit(solution)/shard_map/while/body/eval_jaxpr/ppermute | solution.py:36
  41.6 4.0 %fusion.45 = (f32[4,1024]{1,0:T(4,128)S(1)}, f32[1024,1024,4]{1,0,2:T(8,128)S(1)}) fusion(pred[1024,1024]{0,1:T(8,128)(4,1)S(1)} %broadcast_compare_fusion.3, bf16[1024,4,128]{2,0,1:T(8,128)(2,1)S(1)} %get-tuple-element.400, bf16[1024,128]{1,0:T(8,128)(2,1)S(1)} %collective-permute-done), kind=kOutput, calls=%fused_computation.2.clone.1 | convolution fusion | flops 1086320640 | bytes 19152896 | tf_op jit(solution)/shard_map/while/body/eval_jaxpr/qhd,kd->hqk/dot_general | solution.py:41
  49.4 5.0 %multiply_add_fusion.5 = f32[4,1024,128]{2,1,0:T(8,128)S(1)} fusion(f32[4,1024,128]{2,1,0:T(8,128)S(1)} %copy-done.1, f32[1024,1024,4]{1,0,2:T(8,128)S(1)} %get-tuple-element.356, f32[4,1024]{1,0:T(4,128)S(1)} %max.23, pred[1024,1024]{0,1:T(8,128)(4,1)S(1)} %broadcast_compare_fusion.3, f32[4,1024]{1,0:T(4,128)S(1)} %get-tuple-element.358, ...), kind=kOutput, calls=%fused_computation.9.clone.1 | convolution fusion | flops 1091567616 | bytes 22315008 | tf_op jit(solution)/shard_map/while/body/eval_jaxpr/hqk,kd->hqd/dot_general | solution.py:50
  56.6 6.5 %collective-permute-done = bf16[1024,128]{1,0:T(8,128)(2,1)S(1)} collective-permute-done((bf16[1024,128]{1,0:T(8,128)(2,1)S(1)}, bf16[1024,128]{1,0:T(8,128)(2,1)S(1)}, u32[]{:S(2)}, u32[]{:S(2)}) %collective-permute-start) | collective-permute-done | bytes 262176 | tf_op jit(solution)/shard_map/while/body/eval_jaxpr/ppermute | solution.py:36
  63.1 4.0 %fusion.45 = (f32[4,1024]{1,0:T(4,128)S(1)}, f32[1024,1024,4]{1,0,2:T(8,128)S(1)}) fusion(pred[1024,1024]{0,1:T(8,128)(4,1)S(1)} %broadcast_compare_fusion.3, bf16[1024,4,128]{2,0,1:T(8,128)(2,1)S(1)} %get-tuple-element.400, bf16[1024,128]{1,0:T(8,128)(2,1)S(1)} %collective-permute-done), kind=kOutput, calls=%fused_computation.2.clone.1 | convolution fusion | flops 1086320640 | bytes 19152896 | tf_op jit(solution)/shard_map/while/body/eval_jaxpr/qhd,kd->hqk/dot_general | solution.py:41
  70.9 5.0 %multiply_add_fusion.5 = f32[4,1024,128]{2,1,0:T(8,128)S(1)} fusion(f32[4,1024,128]{2,1,0:T(8,128)S(1)} %copy-done.1, f32[1024,1024,4]{1,0,2:T(8,128)S(1)} %get-tuple-element.356, f32[4,1024]{1,0:T(4,128)S(1)} %max.23, pred[1024,1024]{0,1:T(8,128)(4,1)S(1)} %broadcast_compare_fusion.3, f32[4,1024]{1,0:T(4,128)S(1)} %get-tuple-element.358, ...), kind=kOutput, calls=%fused_computation.9.clone.1 | convolution fusion | flops 1091567616 | bytes 22315008 | tf_op jit(solution)/shard_map/while/body/eval_jaxpr/hqk,kd->hqd/dot_general | solution.py:50
  78.0 6.7 %collective-permute-done = bf16[1024,128]{1,0:T(8,128)(2,1)S(1)} collective-permute-done((bf16[1024,128]{1,0:T(8,128)(2,1)S(1)}, bf16[1024,128]{1,0:T(8,128)(2,1)S(1)}, u32[]{:S(2)}, u32[]{:S(2)}) %collective-permute-start) | collective-permute-done | bytes 262176 | tf_op jit(solution)/shard_map/while/body/eval_jaxpr/ppermute | solution.py:36
  84.6 4.0 %fusion.45 = (f32[4,1024]{1,0:T(4,128)S(1)}, f32[1024,1024,4]{1,0,2:T(8,128)S(1)}) fusion(pred[1024,1024]{0,1:T(8,128)(4,1)S(1)} %broadcast_compare_fusion.3, bf16[1024,4,128]{2,0,1:T(8,128)(2,1)S(1)} %get-tuple-element.400, bf16[1024,128]{1,0:T(8,128)(2,1)S(1)} %collective-permute-done), kind=kOutput, calls=%fused_computation.2.clone.1 | convolution fusion | flops 1086320640 | bytes 19152896 | tf_op jit(solution)/shard_map/while/body/eval_jaxpr/qhd,kd->hqk/dot_general | solution.py:41
  92.5 5.0 %multiply_add_fusion.5 = f32[4,1024,128]{2,1,0:T(8,128)S(1)} fusion(f32[4,1024,128]{2,1,0:T(8,128)S(1)} %copy-done.1, f32[1024,1024,4]{1,0,2:T(8,128)S(1)} %get-tuple-element.356, f32[4,1024]{1,0:T(4,128)S(1)} %max.23, pred[1024,1024]{0,1:T(8,128)(4,1)S(1)} %broadcast_compare_fusion.3, f32[4,1024]{1,0:T(4,128)S(1)} %get-tuple-element.358, ...), kind=kOutput, calls=%fused_computation.9.clone.1 | convolution fusion | flops 1091567616 | bytes 22315008 | tf_op jit(solution)/shard_map/while/body/eval_jaxpr/hqk,kd->hqd/dot_general | solution.py:50
  99.5 6.7 %collective-permute-done = bf16[1024,128]{1,0:T(8,128)(2,1)S(1)} collective-permute-done((bf16[1024,128]{1,0:T(8,128)(2,1)S(1)}, bf16[1024,128]{1,0:T(8,128)(2,1)S(1)}, u32[]{:S(2)}, u32[]{:S(2)}) %collective-permute-start) | collective-permute-done | bytes 262176 | tf_op jit(solution)/shard_map/while/body/eval_jaxpr/ppermute | solution.py:36
  106.2 4.0 %fusion.45 = (f32[4,1024]{1,0:T(4,128)S(1)}, f32[1024,1024,4]{1,0,2:T(8,128)S(1)}) fusion(pred[1024,1024]{0,1:T(8,128)(4,1)S(1)} %broadcast_compare_fusion.3, bf16[1024,4,128]{2,0,1:T(8,128)(2,1)S(1)} %get-tuple-element.400, bf16[1024,128]{1,0:T(8,128)(2,1)S(1)} %collective-permute-done), kind=kOutput, calls=%fused_computation.2.clone.1 | convolution fusion | flops 1086320640 | bytes 19152896 | tf_op jit(solution)/shard_map/while/body/eval_jaxpr/qhd,kd->hqk/dot_general | solution.py:41
  114.0 5.0 %multiply_add_fusion.5 = f32[4,1024,128]{2,1,0:T(8,128)S(1)} fusion(f32[4,1024,128]{2,1,0:T(8,128)S(1)} %copy-done.1, f32[1024,1024,4]{1,0,2:T(8,128)S(1)} %get-tuple-element.356, f32[4,1024]{1,0:T(4,128)S(1)} %max.23, pred[1024,1024]{0,1:T(8,128)(4,1)S(1)} %broadcast_compare_fusion.3, f32[4,1024]{1,0:T(4,128)S(1)} %get-tuple-element.358, ...), kind=kOutput, calls=%fused_computation.9.clone.1 | convolution fusion | flops 1091567616 | bytes 22315008 | tf_op jit(solution)/shard_map/while/body/eval_jaxpr/hqk,kd->hqd/dot_general | solution.py:50
  121.0 6.7 %collective-permute-done = bf16[1024,128]{1,0:T(8,128)(2,1)S(1)} collective-permute-done((bf16[1024,128]{1,0:T(8,128)(2,1)S(1)}, bf16[1024,128]{1,0:T(8,128)(2,1)S(1)}, u32[]{:S(2)}, u32[]{:S(2)}) %collective-permute-start) | collective-permute-done | bytes 262176 | tf_op jit(solution)/shard_map/while/body/eval_jaxpr/ppermute | solution.py:36
  127.7 4.0 %fusion.45 = (f32[4,1024]{1,0:T(4,128)S(1)}, f32[1024,1024,4]{1,0,2:T(8,128)S(1)}) fusion(pred[1024,1024]{0,1:T(8,128)(4,1)S(1)} %broadcast_compare_fusion.3, bf16[1024,4,128]{2,0,1:T(8,128)(2,1)S(1)} %get-tuple-element.400, bf16[1024,128]{1,0:T(8,128)(2,1)S(1)} %collective-permute-done), kind=kOutput, calls=%fused_computation.2.clone.1 | convolution fusion | flops 1086320640 | bytes 19152896 | tf_op jit(solution)/shard_map/while/body/eval_jaxpr/qhd,kd->hqk/dot_general | solution.py:41
  135.5 5.0 %multiply_add_fusion.5 = f32[4,1024,128]{2,1,0:T(8,128)S(1)} fusion(f32[4,1024,128]{2,1,0:T(8,128)S(1)} %copy-done.1, f32[1024,1024,4]{1,0,2:T(8,128)S(1)} %get-tuple-element.356, f32[4,1024]{1,0:T(4,128)S(1)} %max.23, pred[1024,1024]{0,1:T(8,128)(4,1)S(1)} %broadcast_compare_fusion.3, f32[4,1024]{1,0:T(4,128)S(1)} %get-tuple-element.358, ...), kind=kOutput, calls=%fused_computation.9.clone.1 | convolution fusion | flops 1091567616 | bytes 22315008 | tf_op jit(solution)/shard_map/while/body/eval_jaxpr/hqk,kd->hqd/dot_general | solution.py:50
  142.6 6.7 %collective-permute-done = bf16[1024,128]{1,0:T(8,128)(2,1)S(1)} collective-permute-done((bf16[1024,128]{1,0:T(8,128)(2,1)S(1)}, bf16[1024,128]{1,0:T(8,128)(2,1)S(1)}, u32[]{:S(2)}, u32[]{:S(2)}) %collective-permute-start) | collective-permute-done | bytes 262176 | tf_op jit(solution)/shard_map/while/body/eval_jaxpr/ppermute | solution.py:36
  157.1 5.0 %multiply_add_fusion.5 = f32[4,1024,128]{2,1,0:T(8,128)S(1)} fusion(f32[4,1024,128]{2,1,0:T(8,128)S(1)} %copy-done.1, f32[1024,1024,4]{1,0,2:T(8,128)S(1)} %get-tuple-element.356, f32[4,1024]{1,0:T(4,128)S(1)} %max.23, pred[1024,1024]{0,1:T(8,128)(4,1)S(1)} %broadcast_compare_fusion.3, f32[4,1024]{1,0:T(4,128)S(1)} %get-tuple-element.358, ...), kind=kOutput, calls=%fused_computation.9.clone.1 | convolution fusion | flops 1091567616 | bytes 22315008 | tf_op jit(solution)/shard_map/while/body/eval_jaxpr/hqk,kd->hqd/dot_general | solution.py:50
  164.1 6.7 %collective-permute-done = bf16[1024,128]{1,0:T(8,128)(2,1)S(1)} collective-permute-done((bf16[1024,128]{1,0:T(8,128)(2,1)S(1)}, bf16[1024,128]{1,0:T(8,128)(2,1)S(1)}, u32[]{:S(2)}, u32[]{:S(2)}) %collective-permute-start) | collective-permute-done | bytes 262176 | tf_op jit(solution)/shard_map/while/body/eval_jaxpr/ppermute | solution.py:36
  178.6 5.0 %multiply_add_fusion.5 = f32[4,1024,128]{2,1,0:T(8,128)S(1)} fusion(f32[4,1024,128]{2,1,0:T(8,128)S(1)} %copy-done.1, f32[1024,1024,4]{1,0,2:T(8,128)S(1)} %get-tuple-element.356, f32[4,1024]{1,0:T(4,128)S(1)} %max.23, pred[1024,1024]{0,1:T(8,128)(4,1)S(1)} %broadcast_compare_fusion.3, f32[4,1024]{1,0:T(4,128)S(1)} %get-tuple-element.358, ...), kind=kOutput, calls=%fused_computation.9.clone.1 | convolution fusion | flops 1091567616 | bytes 22315008 | tf_op jit(solution)/shard_map/while/body/eval_jaxpr/hqk,kd->hqd/dot_general | solution.py:50
  187.2 15.9 %convolution_convert_fusion = bf16[1024,8192]{1,0:T(8,128)(2,1)} fusion(bf16[1024,512]{0,1:T(8,128)(2,1)S(1)} %bitcast.72, bf16[512,8192]{1,0:T(8,128)(2,1)} %param.14), kind=kOutput, calls=%fused_computation.23 | convolution fusion | flops 8598323200 | bytes 26214400 | tf_op jit(solution)/shard_map/dot_general | solution.py:106
  203.9 156.7 %reduce-scatter.2.cloned.1.call-done = bf16[64,8192]{1,0:T(8,128)(2,1)} async-done(((bf16[1024,8192]{1,0:T(8,128)(2,1)}), bf16[64,8192]{1,0:T(8,128)(2,1)}) %reduce-scatter.2.cloned.1.call-update) | async-done | bytes 1048592 | tf_op jit(solution)/shard_map/reduce_scatter | solution.py:105
  (130 shorter events, 71.6 us)
Async XLA Ops:
  8.5 24.0 %all-to-all-start = ((s32[8,1,1024]{2,1,0:T(1,128)}), s32[8,1,1024]{2,1,0:T(1,128)S(1)}, u32[]{:S(2)}, u32[]{:S(2)}) async-start(s32[8,1,1024]{2,1,0:T(1,128)} %broadcast_in_dim.97), calls=%async_computation | async-start | bytes 65536 | tf_op jit(solution)/shard_map/all_to_all | solution.py:17
  14.8 345.7 %reduce-scatter.2.cloned.1.call-start = ((), (), s32[]{:S(2)}) async-start(), calls=%async_computation.2 | async-start | bytes 17825792 | tf_op jit(solution)/shard_map/reduce_scatter | solution.py:105
  25.9 6.6 %copy-start.3 = (s32[1024]{0:T(1024)S(1)}, s32[1024]{0:T(1024)}, u32[]{:S(2)}) copy-start(s32[1024]{0:T(1024)} %param.13) | copy-start | bytes 12292
  32.5 9.1 %collective-permute-start = (bf16[1024,128]{1,0:T(8,128)(2,1)S(1)}, bf16[1024,128]{1,0:T(8,128)(2,1)S(1)}, u32[]{:S(2)}, u32[]{:S(2)}) collective-permute-start(bf16[1024,128]{1,0:T(8,128)(2,1)S(1)} %get-tuple-element.376), channel_id=1, source_target_pairs={{0,16},{16,32},{32,48},{48,64},{64,80},{80,96},{96,112},{112,0},{1... | collective-permute-start | bytes 786440 | tf_op jit(solution)/shard_map/while/body/eval_jaxpr/ppermute | solution.py:36
  34.0 15.4 %collective-permute-start.1 = (bf16[1024,128]{1,0:T(8,128)(2,1)S(1)}, bf16[1024,128]{1,0:T(8,128)(2,1)S(1)}, u32[]{:S(2)}, u32[]{:S(2)}) collective-permute-start(bf16[1024,128]{1,0:T(8,128)(2,1)S(1)} %get-tuple-element.377), channel_id=1, source_target_pairs={{0,16},{16,32},{32,48},{48,64},{64,80},{80,96},{96,112},{112,0},{1... | collective-permute-start | bytes 786440 | tf_op jit(solution)/shard_map/while/body/eval_jaxpr/ppermute | solution.py:36
  45.6 3.8 %copy-start.1 = (f32[4,1024,128]{2,1,0:T(8,128)S(1)}, f32[4,1024,128]{2,1,0:T(8,128)}, u32[]{:S(2)}) copy-start(f32[4,1024,128]{2,1,0:T(8,128)} %get-tuple-element.380) | copy-start | bytes 6291460 | tf_op jit(solution)/shard_map/while
  55.8 7.3 %collective-permute-start = (bf16[1024,128]{1,0:T(8,128)(2,1)S(1)}, bf16[1024,128]{1,0:T(8,128)(2,1)S(1)}, u32[]{:S(2)}, u32[]{:S(2)}) collective-permute-start(bf16[1024,128]{1,0:T(8,128)(2,1)S(1)} %get-tuple-element.376), channel_id=1, source_target_pairs={{0,16},{16,32},{32,48},{48,64},{64,80},{80,96},{96,112},{112,0},{1... | collective-permute-start | bytes 786440 | tf_op jit(solution)/shard_map/while/body/eval_jaxpr/ppermute | solution.py:36
  55.8 15.1 %collective-permute-start.1 = (bf16[1024,128]{1,0:T(8,128)(2,1)S(1)}, bf16[1024,128]{1,0:T(8,128)(2,1)S(1)}, u32[]{:S(2)}, u32[]{:S(2)}) collective-permute-start(bf16[1024,128]{1,0:T(8,128)(2,1)S(1)} %get-tuple-element.377), channel_id=1, source_target_pairs={{0,16},{16,32},{32,48},{48,64},{64,80},{80,96},{96,112},{112,0},{1... | collective-permute-start | bytes 786440 | tf_op jit(solution)/shard_map/while/body/eval_jaxpr/ppermute | solution.py:36
  67.1 3.8 %copy-start.1 = (f32[4,1024,128]{2,1,0:T(8,128)S(1)}, f32[4,1024,128]{2,1,0:T(8,128)}, u32[]{:S(2)}) copy-start(f32[4,1024,128]{2,1,0:T(8,128)} %get-tuple-element.380) | copy-start | bytes 6291460 | tf_op jit(solution)/shard_map/while
  77.3 7.3 %collective-permute-start = (bf16[1024,128]{1,0:T(8,128)(2,1)S(1)}, bf16[1024,128]{1,0:T(8,128)(2,1)S(1)}, u32[]{:S(2)}, u32[]{:S(2)}) collective-permute-start(bf16[1024,128]{1,0:T(8,128)(2,1)S(1)} %get-tuple-element.376), channel_id=1, source_target_pairs={{0,16},{16,32},{32,48},{48,64},{64,80},{80,96},{96,112},{112,0},{1... | collective-permute-start | bytes 786440 | tf_op jit(solution)/shard_map/while/body/eval_jaxpr/ppermute | solution.py:36
  77.3 15.1 %collective-permute-start.1 = (bf16[1024,128]{1,0:T(8,128)(2,1)S(1)}, bf16[1024,128]{1,0:T(8,128)(2,1)S(1)}, u32[]{:S(2)}, u32[]{:S(2)}) collective-permute-start(bf16[1024,128]{1,0:T(8,128)(2,1)S(1)} %get-tuple-element.377), channel_id=1, source_target_pairs={{0,16},{16,32},{32,48},{48,64},{64,80},{80,96},{96,112},{112,0},{1... | collective-permute-start | bytes 786440 | tf_op jit(solution)/shard_map/while/body/eval_jaxpr/ppermute | solution.py:36
  88.7 3.8 %copy-start.1 = (f32[4,1024,128]{2,1,0:T(8,128)S(1)}, f32[4,1024,128]{2,1,0:T(8,128)}, u32[]{:S(2)}) copy-start(f32[4,1024,128]{2,1,0:T(8,128)} %get-tuple-element.380) | copy-start | bytes 6291460 | tf_op jit(solution)/shard_map/while
  98.8 7.3 %collective-permute-start = (bf16[1024,128]{1,0:T(8,128)(2,1)S(1)}, bf16[1024,128]{1,0:T(8,128)(2,1)S(1)}, u32[]{:S(2)}, u32[]{:S(2)}) collective-permute-start(bf16[1024,128]{1,0:T(8,128)(2,1)S(1)} %get-tuple-element.376), channel_id=1, source_target_pairs={{0,16},{16,32},{32,48},{48,64},{64,80},{80,96},{96,112},{112,0},{1... | collective-permute-start | bytes 786440 | tf_op jit(solution)/shard_map/while/body/eval_jaxpr/ppermute | solution.py:36
  98.8 15.1 %collective-permute-start.1 = (bf16[1024,128]{1,0:T(8,128)(2,1)S(1)}, bf16[1024,128]{1,0:T(8,128)(2,1)S(1)}, u32[]{:S(2)}, u32[]{:S(2)}) collective-permute-start(bf16[1024,128]{1,0:T(8,128)(2,1)S(1)} %get-tuple-element.377), channel_id=1, source_target_pairs={{0,16},{16,32},{32,48},{48,64},{64,80},{80,96},{96,112},{112,0},{1... | collective-permute-start | bytes 786440 | tf_op jit(solution)/shard_map/while/body/eval_jaxpr/ppermute | solution.py:36
  110.2 3.8 %copy-start.1 = (f32[4,1024,128]{2,1,0:T(8,128)S(1)}, f32[4,1024,128]{2,1,0:T(8,128)}, u32[]{:S(2)}) copy-start(f32[4,1024,128]{2,1,0:T(8,128)} %get-tuple-element.380) | copy-start | bytes 6291460 | tf_op jit(solution)/shard_map/while
  120.4 7.3 %collective-permute-start = (bf16[1024,128]{1,0:T(8,128)(2,1)S(1)}, bf16[1024,128]{1,0:T(8,128)(2,1)S(1)}, u32[]{:S(2)}, u32[]{:S(2)}) collective-permute-start(bf16[1024,128]{1,0:T(8,128)(2,1)S(1)} %get-tuple-element.376), channel_id=1, source_target_pairs={{0,16},{16,32},{32,48},{48,64},{64,80},{80,96},{96,112},{112,0},{1... | collective-permute-start | bytes 786440 | tf_op jit(solution)/shard_map/while/body/eval_jaxpr/ppermute | solution.py:36
  120.4 15.1 %collective-permute-start.1 = (bf16[1024,128]{1,0:T(8,128)(2,1)S(1)}, bf16[1024,128]{1,0:T(8,128)(2,1)S(1)}, u32[]{:S(2)}, u32[]{:S(2)}) collective-permute-start(bf16[1024,128]{1,0:T(8,128)(2,1)S(1)} %get-tuple-element.377), channel_id=1, source_target_pairs={{0,16},{16,32},{32,48},{48,64},{64,80},{80,96},{96,112},{112,0},{1... | collective-permute-start | bytes 786440 | tf_op jit(solution)/shard_map/while/body/eval_jaxpr/ppermute | solution.py:36
  131.7 3.8 %copy-start.1 = (f32[4,1024,128]{2,1,0:T(8,128)S(1)}, f32[4,1024,128]{2,1,0:T(8,128)}, u32[]{:S(2)}) copy-start(f32[4,1024,128]{2,1,0:T(8,128)} %get-tuple-element.380) | copy-start | bytes 6291460 | tf_op jit(solution)/shard_map/while
  141.9 7.3 %collective-permute-start = (bf16[1024,128]{1,0:T(8,128)(2,1)S(1)}, bf16[1024,128]{1,0:T(8,128)(2,1)S(1)}, u32[]{:S(2)}, u32[]{:S(2)}) collective-permute-start(bf16[1024,128]{1,0:T(8,128)(2,1)S(1)} %get-tuple-element.376), channel_id=1, source_target_pairs={{0,16},{16,32},{32,48},{48,64},{64,80},{80,96},{96,112},{112,0},{1... | collective-permute-start | bytes 786440 | tf_op jit(solution)/shard_map/while/body/eval_jaxpr/ppermute | solution.py:36
  141.9 15.1 %collective-permute-start.1 = (bf16[1024,128]{1,0:T(8,128)(2,1)S(1)}, bf16[1024,128]{1,0:T(8,128)(2,1)S(1)}, u32[]{:S(2)}, u32[]{:S(2)}) collective-permute-start(bf16[1024,128]{1,0:T(8,128)(2,1)S(1)} %get-tuple-element.377), channel_id=1, source_target_pairs={{0,16},{16,32},{32,48},{48,64},{64,80},{80,96},{96,112},{112,0},{1... | collective-permute-start | bytes 786440 | tf_op jit(solution)/shard_map/while/body/eval_jaxpr/ppermute | solution.py:36
  163.4 7.3 %collective-permute-start = (bf16[1024,128]{1,0:T(8,128)(2,1)S(1)}, bf16[1024,128]{1,0:T(8,128)(2,1)S(1)}, u32[]{:S(2)}, u32[]{:S(2)}) collective-permute-start(bf16[1024,128]{1,0:T(8,128)(2,1)S(1)} %get-tuple-element.376), channel_id=1, source_target_pairs={{0,16},{16,32},{32,48},{48,64},{64,80},{80,96},{96,112},{112,0},{1... | collective-permute-start | bytes 786440 | tf_op jit(solution)/shard_map/while/body/eval_jaxpr/ppermute | solution.py:36
  163.4 15.1 %collective-permute-start.1 = (bf16[1024,128]{1,0:T(8,128)(2,1)S(1)}, bf16[1024,128]{1,0:T(8,128)(2,1)S(1)}, u32[]{:S(2)}, u32[]{:S(2)}) collective-permute-start(bf16[1024,128]{1,0:T(8,128)(2,1)S(1)} %get-tuple-element.377), channel_id=1, source_target_pairs={{0,16},{16,32},{32,48},{48,64},{64,80},{80,96},{96,112},{112,0},{1... | collective-permute-start | bytes 786440 | tf_op jit(solution)/shard_map/while/body/eval_jaxpr/ppermute | solution.py:36
  203.1 157.4 %copy-start = (bf16[64,8192]{1,0:T(8,128)(2,1)S(1)}, bf16[64,8192]{1,0:T(8,128)(2,1)}, u32[]{:S(2)}) copy-start(bf16[64,8192]{1,0:T(8,128)(2,1)} %param.15) | copy-start | bytes 3145732
  203.1 160.1 %copy-start.4 = (f32[8192]{0:T(1024)S(1)}, f32[8192]{0:T(1024)}, u32[]{:S(2)}) copy-start(f32[8192]{0:T(1024)} %param.16) | copy-start | bytes 98308
  (9 other events, 17.0 us)
Sparse Core Ops, SparseCore 0:
  203.3 157.2 reduce-scatter.1
where the time goes:
time: 373 us
  waiting for transfers between devices  202 us (54%)
  matrix products  88.3 us (24%)
  other arithmetic  41.2 us (11%)
  local copies, waits for them, and re-layouts  16.2 us (4%)
  between operations  14.9 us (4%)
  starting transfers between devices  9.29 us (2%)
    reduce_scatter x1, waiting for transfers between devices, shards(): lax.psum_scatter(jnp.dot(attended, out_weight, preferred_element_type=jnp...  157 us
    ppermute x14, waiting for transfers between devices, shifted(): return lax.ppermute(value, axis, pairs)  45.5 us
    dot_general x8, matrix products, update_block(): jnp.einsum('hqk,kd->hqd', weights, value_blk, preferred_element_type=jnp....  41 us
    dot_general x8, matrix products, update_block(): jnp.einsum('qhd,kd->hqk', query_blk, key_blk, preferred_element_type=jnp....  31.4 us
    reduce_sum x8, other arithmetic, update_block(): run_total = run_total * factor + jnp.sum(expo, axis=2)  29.3 us
    dot_general x1, matrix products, shards(): jnp.dot(attended, out_weight, preferred_element_type=jnp.float32)  15.9 us
    while x49, local copies, waits for them, and re-layouts  9.66 us
  transfers between devices with their start and end apart: 16, of which 8 were waited for; matrix products, arithmetic and copies ran while one was open for 20% of the time, Pallas kernels for 0%

commit v1 on v0

v1 whole, which is shorter than its diff:
```python
import math

import jax
import jax.numpy as jnp
from jax import lax
from jax.experimental import pallas as pl
from jax.experimental.pallas import tpu as pltpu
from jax.sharding import PartitionSpec as P

HD = 128
SPAN = 512
ROWS = 64
WIDTH = 8192
CHUNKS = 4
TILE = 512
NEG = -1e30
MESH = pl.DeviceIdType.MESH
bf16 = jnp.bfloat16
f32 = jnp.float32


def kernel(
    q_hbm, k_hbm, v_hbm, pos_hbm, w_hbm, res_hbm, gain_hbm, scale_ref,
    hidden_ref, clipped_ref,
    wbuf, kv, vt, qbuf, posall, qt, acc, m_sc, l_sc, att, send, recv, fin, zrecv, summed, res, gain,
    lsem, qsem, wsem, gs, gr, ds, dr, ps, pr, xs, xr, zs, zr,
):
    ctx = lax.axis_index("ctx")
    tp = lax.axis_index("tp")
    zlo, y = ctx // 4, ctx % 4
    zhi, x, core = tp // 8, (tp // 2) % 4, tp % 2
    group = tp // 2
    yup, ydn = (y + 1) % 4, (y + 3) % 4
    zother = 1 - zlo

    def at_ctx(zl, yy):
        return (zl * 4 + yy, tp)

    def at_tp(zh, xx, cc):
        return (ctx, zh * 8 + xx * 2 + cc)

    mate = at_tp(zhi, x, 1 - core)
    xup, xdn = at_tp(zhi, (x + 1) % 4, core), at_tp(zhi, (x + 3) % 4, core)
    zmate = at_tp(1 - zhi, x, core)

    def rcopy(src, dst, ssem, rsem, dev):
        return pltpu.make_async_remote_copy(
            src_ref=src, dst_ref=dst, send_sem=ssem, recv_sem=rsem, device_id=dev, device_id_type=MESH
        )

    load_k = pltpu.make_async_copy(
        k_hbm.at[:, :, pl.ds(pl.multiple_of(group * HD, HD), HD)], kv.at[0, pl.ds(2 * ctx, 2)], lsem.at[0]
    )
    load_v = pltpu.make_async_copy(
        v_hbm.at[:, :, pl.ds(pl.multiple_of(group * HD, HD), HD)], kv.at[1, pl.ds(2 * ctx, 2)], lsem.at[1]
    )
    load_p = pltpu.make_async_copy(pos_hbm, posall.at[ctx], lsem.at[2])
    qcol = pl.ds(pl.multiple_of(core * 512, 512), 512)
    load_q = pltpu.make_async_copy(q_hbm.at[:, core], qbuf.at[:, :, qcol], lsem.at[3])
    load_w = pltpu.make_async_copy(w_hbm, wbuf.at[core], lsem.at[4])
    load_r = pltpu.make_async_copy(res_hbm, res, lsem.at[5])
    load_g = pltpu.make_async_copy(gain_hbm, gain, lsem.at[6])
    for c in (load_k, load_v, load_p, load_q, load_w, load_r, load_g):
        c.start()

    barrier = pltpu.get_barrier_semaphore()
    peers = [mate, xup, xdn, zmate] + [((ctx + i) % 8, tp) for i in range(1, 8)]
    for dev in peers:
        pl.semaphore_signal(barrier, inc=1, device_id=dev, device_id_type=MESH)
    pl.semaphore_wait(barrier, len(peers))

    def item(what, zl, yy):
        return kv.at[what, pl.ds((zl * 4 + yy) * 2, 2)]

    def half(what, zl, yy, part):
        return kv.at[what, pl.ds((zl * 4 + yy) * 2 + part, 1)]

    started = []

    def start(copy):
        copy.start()
        started.append(copy)

    load_k.wait()
    load_v.wait()
    own = item(core, zlo, y)
    start(rcopy(own, own, gs.at[0], gr.at[0], at_ctx(zother, y)))
    start(rcopy(own, own, gs.at[1], gr.at[1], at_ctx(zlo, yup)))
    start(rcopy(own, own, gs.at[2], gr.at[2], at_ctx(zlo, ydn)))
    load_p.wait()
    for i in range(1, 8):
        start(rcopy(posall.at[ctx], posall.at[ctx], ps.at[i - 1], pr.at[i - 1], ((ctx + i) % 8, tp)))
    start(rcopy(q_hbm.at[:, 1 - core], qbuf.at[:, :, qcol], qsem.at[0], qsem.at[1], mate))
    start(rcopy(w_hbm, wbuf.at[core], wsem.at[0], wsem.at[1], mate))

    def arrived(ref, sem, dev):
        rcopy(ref, ref, gs.at[0], sem, dev).wait_recv()

    def pass_on(ref, n):
        start(rcopy(ref, ref, ds.at[n], dr.at[n], mate))

    got = item(core, zother, y)
    arrived(got, gr.at[0], mate)
    start(rcopy(got, got, gs.at[3], gr.at[3], at_ctx(zlo, yup)))
    start(rcopy(got, got, gs.at[4], gr.at[4], at_ctx(zlo, ydn)))
    pass_on(got, 0)
    for n, zl in ((1, zlo), (3, zother)):
        below, above = item(core, zl, ydn), item(core, zl, yup)
        arrived(below, gr.at[n], mate)
        h = half(core, zl, ydn, 0)
        start(rcopy(h, h, gs.at[n + 4], gr.at[n + 4], at_ctx(zlo, yup)))
        pass_on(below, n)
        arrived(above, gr.at[n + 1], mate)
        h = half(core, zl, yup, 1)
        start(rcopy(h, h, gs.at[n + 5], gr.at[n + 5], at_ctx(zlo, ydn)))
        pass_on(above, n + 1)
    yfar = (y + 2) % 4
    for n, zl in ((5, zlo), (7, zother)):
        for part in range(2):
            h = half(core, zl, yfar, part)
            arrived(h, gr.at[n + part], mate)
            pass_on(h, n + part)
    what = 1 - core
    arrived(item(what, zother, y), dr.at[0], mate)
    for n, zl in ((1, zlo), (3, zother)):
        arrived(item(what, zl, ydn), dr.at[n], mate)
        arrived(item(what, zl, yup), dr.at[n + 1], mate)
    for n, zl in ((5, zlo), (7, zother)):
        for part in range(2):
            arrived(half(what, zl, yfar, part), dr.at[n + part], mate)
    for i in range(1, 8):
        src = posall.at[(ctx + 8 - i) % 8]
        rcopy(src, src, ps.at[0], pr.at[i - 1], mate).wait_recv()
    load_q.wait()
    qother = qbuf.at[:, :, pl.ds(pl.multiple_of((1 - core) * 512, 512), 512)]
    rcopy(qother, qother, qsem.at[0], qsem.at[1], mate).wait_recv()

    @pl.loop(0, 16)
    def _(i):
        vt[i] = kv[1, i].T

    score_scale = math.log2(math.e) / math.sqrt(HD)

    def attend(tile, key_span, bias, first, diag):
        keys = kv[0, key_span]
        s = jnp.dot(
            jnp.concatenate([keys, keys], axis=1), qt[tile], preferred_element_type=f32
        )
        if diag is not None:
            s = jnp.where(diag, s, NEG)
        top = jnp.max(s, axis=0, keepdims=True)
        if first:
            new = top
            p = jnp.exp2(s - new)
            l_sc[tile] = jnp.sum(p, axis=0, keepdims=True)
            acc[tile] = jnp.dot(vt[key_span], p.astype(bf16), preferred_element_type=f32)
        else:
            old = m_sc[tile]
            new = jnp.maximum(old, top + bias)
            p = jnp.exp2(s - (new - bias))
            alpha = jnp.exp2(old - new)
            l_sc[tile] = l_sc[tile] * alpha + jnp.sum(p, axis=0, keepdims=True)
            acc[tile] = acc[tile] * alpha + jnp.dot(vt[key_span], p.astype(bf16), preferred_element_type=f32)
        m_sc[tile] = new

    def start_of(span):
        row = posall[span // 2, pl.ds(pl.multiple_of((span % 2) * 8, 8), 8), :][0:1]
        return jnp.concatenate([row, row], axis=1)

    own_spans = (2 * ctx, 2 * ctx + 1)
    own_starts = [start_of(span) for span in own_spans]

    def attention(dests):
        for tile in range(4):
            way, hh = tile // 2, tile % 2
            rows = qbuf[way * 4 + dests[way]]
            stack = jnp.concatenate(
                [rows[:, (hh * 4 + h) * HD : (hh * 4 + h + 1) * HD] for h in range(4)], axis=0
            )
            qf = stack.astype(f32).T * score_scale
            hi = qf.astype(bf16)
            lo = (qf - hi.astype(f32)).astype(bf16)
            qt[tile] = jnp.concatenate([hi, lo], axis=0)
        for tile in range(4):
            way = tile // 2
            key_at = lax.broadcasted_iota(jnp.int32, (SPAN, 256), 0)
            row_at = lax.broadcasted_iota(jnp.int32, (SPAN, 256), 1) % ROWS
            diag = key_at <= row_at + (dests[way] * 128 + core * ROWS)
            attend(tile, own_spans[way], None, True, diag)

        @pl.loop(1, 16)
        def _(i):
            for tile in range(4):
                way = tile // 2
                span = (own_spans[way] + i) % 16
                bias = jnp.where(start_of(span) < own_starts[way], 0.0, NEG).astype(f32)
                attend(tile, span, bias, False, None)

        for tile in range(4):
            way, hh = tile // 2, tile % 2
            out = (acc[tile] / l_sc[tile]).T.astype(bf16)
            for h in range(4):
                head = hh * 4 + h
                att[way * ROWS : (way + 1) * ROWS, head * HD : (head + 1) * HD] = out[h * ROWS : (h + 1) * ROWS]

    per = WIDTH // CHUNKS
    for step in range(4):
        dests = ((x + 3 - step) % 4, (x + 1 + step) % 4)
        attention(dests)
        if step == 0:
            load_w.wait()
            rcopy(w_hbm, wbuf.at[1 - core], wsem.at[0], wsem.at[1], mate).wait_recv()
        for chunk in range(CHUNKS):
            piece = pl.ds(chunk * per, per)
            if step > 0:
                for way in range(2):
                    r = recv.at[way, step - 1, :, piece]
                    rcopy(r, r, xs.at[0, 0, 0], xr.at[way, step - 1, chunk], mate).wait_recv()

            @pl.loop(0, per // TILE)
            def _(t):
                cols = pl.ds(pl.multiple_of(chunk * per + t * TILE, TILE), TILE)
                r = jnp.dot(att[:, :512], wbuf[0, :, cols], preferred_element_type=f32)
                r += jnp.dot(att[:, 512:], wbuf[1, :, cols], preferred_element_type=f32)
                up, down = r[:ROWS], r[ROWS:]
                if step > 0:
                    up += recv[0, step - 1, :, cols].astype(f32)
                    down += recv[1, step - 1, :, cols].astype(f32)
                if step < 3:
                    send[0, step, :, cols] = up.astype(bf16)
                    send[1, step, :, cols] = down.astype(bf16)
                else:
                    mine = zhi == 0
                    summed[:, cols] = jnp.where(mine, up, down)
                    fin[:, cols] = jnp.where(mine, down, up).astype(bf16)

            if step < 3:
                for way, dev in ((0, xup), (1, xdn)):
                    start(
                        rcopy(
                            send.at[way, step, :, piece], recv.at[way, step, :, piece],
                            xs.at[way, step, chunk], xr.at[way, step, chunk], dev,
                        )
                    )
            else:
                start(rcopy(fin.at[:, piece], zrecv.at[:, piece], zs.at[chunk], zr.at[chunk], zmate))

    load_r.wait()
    load_g.wait()
    squares = jnp.zeros((ROWS, TILE), f32)
    for chunk in range(CHUNKS):
        piece = zrecv.at[:, pl.ds(chunk * per, per)]
        rcopy(piece, piece, zs.at[0], zr.at[chunk], zmate).wait_recv()
        for t in range(per // TILE):
            cols = slice(chunk * per + t * TILE, chunk * per + (t + 1) * TILE)
            total = summed[:, cols] + zrecv[:, cols].astype(f32) + res[:, cols].astype(f32)
            summed[:, cols] = total
            hidden_ref[:, cols] = total.astype(bf16)
            squares += total * total
    inv_rms = lax.rsqrt(jnp.sum(squares, axis=1, keepdims=True) * (1.0 / WIDTH) + 1e-5)
    limit = 448.0 * scale_ref[0]
    for t in range(WIDTH // TILE):
        cols = slice(t * TILE, (t + 1) * TILE)
        value = summed[:, cols] * inv_rms * gain[:, cols]
        clipped_ref[:, cols] = jnp.minimum(jnp.maximum(value, -limit), limit).astype(bf16)
    for copy in started:
        copy.wait_send()


def shards(queries, context_keys, context_values, positions, out_weight, residual_in, norm_gain, static_scale):
    starts = jnp.broadcast_to(positions.reshape(2, SPAN)[:, :1, None], (2, 8, 128)).reshape(16, 128)
    dma = pltpu.SemaphoreType.DMA
    out = jax.ShapeDtypeStruct((ROWS, WIDTH), bf16)
    anywhere = pl.BlockSpec(memory_space=pl.ANY)
    return pl.pallas_call(
        kernel,
        out_shape=(out, out),
        in_specs=[anywhere] * 7 + [pl.BlockSpec(memory_space=pltpu.SMEM)],
        out_specs=(pl.BlockSpec(memory_space=pltpu.VMEM),) * 2,
        scratch_shapes=[
            pltpu.VMEM((2, 512, WIDTH), bf16),
            pltpu.VMEM((2, 16, SPAN, HD), bf16),
            pltpu.VMEM((16, HD, SPAN), bf16),
            pltpu.VMEM((8, ROWS, 1024), bf16),
            pltpu.VMEM((8, 16, 128), jnp.int32),
            pltpu.VMEM((4, 2 * HD, 256), bf16),
            pltpu.VMEM((4, HD, 256), f32),
            pltpu.VMEM((4, 1, 256), f32),
            pltpu.VMEM((4, 1, 256), f32),
            pltpu.VMEM((2 * ROWS, 1024), bf16),
            pltpu.VMEM((2, 3, ROWS, WIDTH), bf16),
            pltpu.VMEM((2, 3, ROWS, WIDTH), bf16),
            pltpu.VMEM((ROWS, WIDTH), bf16),
            pltpu.VMEM((ROWS, WIDTH), bf16),
            pltpu.VMEM((ROWS, WIDTH), f32),
            pltpu.VMEM((ROWS, WIDTH), bf16),
            pltpu.VMEM((1, WIDTH), f32),
            dma((7,)), dma((2,)), dma((2,)), dma((9,)), dma((9,)), dma((9,)), dma((9,)), dma((7,)), dma((7,)),
            dma((2, 3, CHUNKS)), dma((2, 3, CHUNKS)), dma((CHUNKS,)), dma((CHUNKS,)),
        ],
        compiler_params=pltpu.CompilerParams(
            collective_id=0, has_side_effects=True, vmem_limit_bytes=62 * 1024 * 1024
        ),
    )(
        queries.reshape(8, 2, ROWS, 512),
        context_keys.reshape(2, SPAN, 1024),
        context_values.reshape(2, SPAN, 1024),
        starts,
        out_weight,
        residual_in,
        norm_gain.reshape(1, WIDTH),
        static_scale,
    )


def solution(mesh):
    return jax.shard_map(
        shards,
        mesh=mesh,
        in_specs=(
            P("ctx", "tp"),
            P("ctx", None),
            P("ctx", None),
            P("ctx"),
            P("tp", None),
            P(("ctx", "tp"), None),
            P(),
            P(),
        ),
        out_specs=(P(("ctx", "tp"), None), P(("ctx", "tp"), None)),
        check_vma=False,
    )
```

time: 373 us -> 189 us (0.51)
  waiting for transfers between devices: 202 us -> 0 us
  Pallas kernels: 0 us -> 183 us
  matrix products: 88.3 us -> 0 us
  other arithmetic: 41.2 us -> 0 us
  between operations: 14.9 us -> 1.3 us
  local copies, waits for them, and re-layouts: 16.2 us -> 4.97 us
  starting transfers between devices: 9.29 us -> 0 us
    pallas_call x0 -> x1, Pallas kernels: none -> 183 us  [shards(): pl.pallas_call(kernel, out_shape=(out, out), in_specs=[anywhere] * 7 + [p...]
    reduce_scatter x1 -> x0, waiting for transfers between devices: 157 us -> none  [shards(): lax.psum_scatter(jnp.dot(attended, out_weight, preferred_element_type=jnp...]
    dot_general x17 -> x0, matrix products: 88.3 us -> none  [the longest x8 41 us: update_block(): jnp.einsum('hqk,kd->hqd', weights, value_blk, preferred_element_type=jnp....]
    ppermute x14 -> x0, waiting for transfers between devices: 45.5 us -> none  [shifted(): return lax.ppermute(value, axis, pairs)]
    reduce_sum x9 -> x0, other arithmetic: 32 us -> none  [the longest x8 29.3 us: update_block(): run_total = run_total * factor + jnp.sum(expo, axis=2)]
    while x51 -> x0, local copies, waits for them, and re-layouts: 12.3 us -> none
    all_to_all x1 -> x0, starting transfers between devices: 6.36 us -> none  [sent_to_all(): lax.all_to_all(jnp.broadcast_to(array[None], (count, *array.shape)), axis...]
    le x8 -> x0, other arithmetic: 5.98 us -> none  [update_block(): allowed = key_pos[None, None, :] <= query_pos[None, :, None]]
  transfers between devices with their start and end apart: 16 -> 0, of which waited for: 8 -> 0; matrix products, arithmetic and copies ran while one was open for 20% -> 0% of each run, Pallas kernels for 0% -> 0%
where the time goes in v1:
time: 189 us
  Pallas kernels  183 us (97%)
  local copies, waits for them, and re-layouts  4.97 us (3%)
    pallas_call x1, Pallas kernels, shards(): pl.pallas_call(kernel, out_shape=(out, out), in_specs=[anywhere] * 7 + [p...  183 us

profile of v1, /device:TPU:1, one launch (start us, length us, event | category | flops | bytes accessed | tf_op | source)
XLA Modules:
  0.0 189.3 jit_solution(81432533099398616)
XLA Ops:
  1.3 0.7 reshape.25
  2.0 0.1 slice_reduce_fusion
  2.1 0.1 broadcast_in_dim.13
  2.2 0.1 broadcast_in_dim.14
  2.2 0.7 broadcast_in_dim.15.pos_hbm
  2.9 183.1 %shard_map.95 = (bf16[64,8192]{1,0:T(8,128)(2,1)}, bf16[64,8192]{1,0:T(8,128)(2,1)}) custom-call(bf16[8,2,64,512]{3,2,1,0:T(8,128)(2,1)} %bitcast.6, bf16[2,512,1024]{2,1,0:T(8,128)(2,1)} %bitcast.4, bf16[2,512,1024]{2,1,0:T(8,128)(2,1)} %bitcast.5, s32[16,128]{1,0:T(8,128)} %broadcast_in_dim.15.pos_hbm, bf16[512,8192]{1,0:T(8,128)(2,1)} %w_hbm.1, ...), custom_call_target="tpu_custom_call" | custom-call | tf_op jit(solution)/shard_map/pallas_call | solution.py:275
  186.0 0.0 copy-start
  186.0 2.4 %copy.13 = bf16[64,8192]{1,0:T(8,128)(2,1)} copy(bf16[64,8192]{1,0:T(8,128)(2,1)} %get-tuple-element.4) | data formatting | bytes 2097152
  188.3 0.0 copy-done
  188.3 1.0 copy.14
Async XLA Ops:
  186.0 2.4 %copy-start = (bf16[64,8192]{1,0:T(8,128)(2,1)S(1)}, bf16[64,8192]{1,0:T(8,128)(2,1)}, u32[]{:S(2)}) copy-start(bf16[64,8192]{1,0:T(8,128)(2,1)} %get-tuple-element.5) | copy-start | bytes 3145732

commit v2 on v1

v2 whole, which is shorter than its diff:
```python
import math

import jax
import jax.numpy as jnp
from jax import lax
from jax.experimental import pallas as pl
from jax.experimental.pallas import tpu as pltpu
from jax.sharding import PartitionSpec as P

HD = 128
SPAN = 512
ROWS = 64
WIDTH = 8192
TILE = 512
A_COLS = 5120
A_CHUNKS = 5
A_PER = A_COLS // A_CHUNKS
B_COLS = (WIDTH - A_COLS) // 2
NEG = -1e30
MESH = pl.DeviceIdType.MESH
bf16 = jnp.bfloat16
f32 = jnp.float32


def kernel(
    q_hbm, k_hbm, v_hbm, pos_hbm, w_hbm, res_hbm, gain_hbm, scale_ref,
    hidden_ref, clipped_ref,
    wbuf, kv, foreign, vt, qbuf, posall, qt, acc, m_sc, a_sc, t_sc, s_sc, p_sc, att,
    send, recv, zsend, zgot, bown, bsend, brecv, fin, zrecv, summed, res, gain,
    lsem, qsem, wsem, gs, gr, ds, dr, ps, pr, xs, xr, bzs, bzr, bxs, bxr, zs, zr,
):
    ctx = lax.axis_index("ctx")
    tp = lax.axis_index("tp")
    zlo, y = ctx // 4, ctx % 4
    zhi, x, core = tp // 8, (tp // 2) % 4, tp % 2
    group = tp // 2
    yup, ydn, yfar = (y + 1) % 4, (y + 3) % 4, (y + 2) % 4
    zother = 1 - zlo

    def at_ctx(zl, yy):
        return (zl * 4 + yy, tp)

    def at_tp(zh, xx, cc):
        return (ctx, zh * 8 + xx * 2 + cc)

    mate = at_tp(zhi, x, 1 - core)
    xup, xdn = at_tp(zhi, (x + 1) % 4, core), at_tp(zhi, (x + 3) % 4, core)
    zmate = at_tp(1 - zhi, x, core)
    zpair = at_ctx(zother, y)
    znext = (zother * 4 + y, (1 - zhi) * 8 + x * 2 + core)
    yabove, ybelow = at_ctx(zlo, yup), at_ctx(zlo, ydn)

    def rcopy(src, dst, ssem, rsem, dev):
        return pltpu.make_async_remote_copy(
            src_ref=src, dst_ref=dst, send_sem=ssem, recv_sem=rsem, device_id=dev, device_id_type=MESH
        )

    def heads(g):
        return pl.ds(pl.multiple_of(g * HD, HD), HD)

    far_group = (1 - zhi) * 4 + x
    qcol = pl.ds(pl.multiple_of(core * 512, 512), 512)
    loads = []
    for n, (source, target) in enumerate((
        (k_hbm.at[:, :, heads(group)], kv.at[0, pl.ds(2 * ctx, 2)]),
        (v_hbm.at[:, :, heads(group)], kv.at[1, pl.ds(2 * ctx, 2)]),
        (k_hbm.at[pl.ds(1, 1), :, heads(far_group)], foreign.at[0]),
        (v_hbm.at[pl.ds(1, 1), :, heads(far_group)], foreign.at[1]),
        (pos_hbm, posall.at[ctx]),
        (q_hbm.at[:, core], qbuf.at[:, :, qcol]),
        (w_hbm, wbuf.at[core]),
        (res_hbm, res),
        (gain_hbm, gain),
    )):
        copy = pltpu.make_async_copy(source, target, lsem.at[n])
        copy.start()
        loads.append(copy)

    barrier = pltpu.get_barrier_semaphore()
    peers = [mate, xup, xdn, zmate, znext] + [((ctx + i) % 8, tp) for i in range(1, 8)]
    for dev in peers:
        pl.semaphore_signal(barrier, inc=1, device_id=dev, device_id_type=MESH)
    pl.semaphore_wait(barrier, len(peers))

    def item(what, zl, yy):
        return kv.at[what, pl.ds((zl * 4 + yy) * 2, 2)]

    def half(what, zl, yy, part):
        return kv.at[what, pl.ds((zl * 4 + yy) * 2 + part, 1)]

    started = []

    def start(copy):
        copy.start()
        started.append(copy)

    waiting = [5, 6, 0, 1, 2, 3, 4, 7]

    def weights_on(count):
        for _ in range(count):
            if waiting:
                n = waiting.pop(0)
                piece = pl.ds(n * 1024, 1024)
                start(rcopy(w_hbm.at[:, piece], wbuf.at[core, :, piece], wsem.at[0, n], wsem.at[1, n], mate))

    here = set()

    def weights_here(*pieces):
        for n in pieces:
            if n not in here:
                here.add(n)
                arrived(wbuf.at[1 - core, :, pl.ds(n * 1024, 1024)], wsem.at[1, n])

    def send_on(ref, n, dev):
        start(rcopy(ref, ref, gs.at[n], gr.at[n], dev))

    def arrived(ref, sem):
        rcopy(ref, ref, gs.at[0], sem, mate).wait_recv()

    def pass_on(ref, n):
        start(rcopy(ref, ref, ds.at[n], dr.at[n], mate))

    for n in range(4):
        loads[n].wait()
    first = half(core, zlo, y, 0)
    send_on(first, 0, zpair)
    start(rcopy(foreign.at[core], half(core, zlo, y, 1), gs.at[1], gr.at[1], znext))
    own = item(core, zlo, y)
    send_on(own, 2, yabove)
    send_on(own, 3, ybelow)
    start(rcopy(q_hbm.at[:, 1 - core], qbuf.at[:, :, qcol], qsem.at[0], qsem.at[1], mate))
    loads[4].wait()
    for i in range(1, 8):
        start(rcopy(posall.at[ctx], posall.at[ctx], ps.at[i - 1], pr.at[i - 1], ((ctx + i) % 8, tp)))
    weights_on(2)

    order = [
        zlo * 4 + y, zother * 4 + y, zlo * 4 + ydn, zlo * 4 + yup,
        zother * 4 + ydn, zother * 4 + yup, zlo * 4 + yfar, zother * 4 + yfar,
    ]

    def gathered(n):
        if n == 1:
            got = half(core, zother, y, 1)
            arrived(got, gr.at[1])
            send_on(got, 4, yabove)
            send_on(got, 5, ybelow)
            pass_on(got, 1)
            got = half(core, zother, y, 0)
            arrived(got, gr.at[0])
            pass_on(got, 0)
            weights_on(1)
        elif n == 2:
            got = item(core, zlo, ydn)
            arrived(got, gr.at[2])
            send_on(half(core, zlo, ydn, 0), 6, yabove)
            send_on(half(core, zlo, ydn, 0), 7, zpair)
            pass_on(got, 2)
            got = item(core, zlo, yup)
            arrived(got, gr.at[3])
            send_on(half(core, zlo, yup, 1), 8, ybelow)
            send_on(half(core, zlo, yup, 0), 9, zpair)
            pass_on(got, 3)
            weights_on(2)
        elif n == 4:
            below, above = half(core, zother, ydn, 1), half(core, zother, yup, 1)
            arrived(below, gr.at[4])
            arrived(above, gr.at[5])
            lower = core == 0
            source = jnp.where(lower, ydn, yup)
            target = at_ctx(zlo, jnp.where(lower, yup, ydn))
            send_on(half(core, zother, source, 1), 10, target)
            pass_on(below, 4)
            pass_on(above, 5)
            got = half(core, zlo, yfar, 0)
            arrived(got, gr.at[6])
            send_on(got, 11, zpair)
            pass_on(got, 6)
            got = half(core, zlo, yfar, 1)
            arrived(got, gr.at[8])
            pass_on(got, 8)
            weights_on(1)
        elif n == 5:
            got = half(core, zother, ydn, 0)
            arrived(got, gr.at[7])
            pass_on(got, 7)
            got = half(core, zother, yup, 0)
            arrived(got, gr.at[9])
            pass_on(got, 9)
            weights_on(2)
        elif n == 7:
            got = half(core, zother, yfar, 1)
            arrived(got, gr.at[10])
            pass_on(got, 10)
            got = half(core, zother, yfar, 0)
            arrived(got, gr.at[11])
            pass_on(got, 11)

    def ready(n):
        what = 1 - core
        if n == 1:
            arrived(half(what, zother, y, 1), dr.at[1])
            arrived(half(what, zother, y, 0), dr.at[0])
        elif n == 2:
            arrived(item(what, zlo, ydn), dr.at[2])
        elif n == 3:
            arrived(item(what, zlo, yup), dr.at[3])
        elif n == 4:
            arrived(half(what, zother, ydn, 1), dr.at[4])
            arrived(half(what, zother, ydn, 0), dr.at[7])
        elif n == 5:
            arrived(half(what, zother, yup, 1), dr.at[5])
            arrived(half(what, zother, yup, 0), dr.at[9])
        elif n == 6:
            arrived(half(what, zlo, yfar, 0), dr.at[6])
            arrived(half(what, zlo, yfar, 1), dr.at[8])
        elif n == 7:
            arrived(half(what, zother, yfar, 1), dr.at[10])
            arrived(half(what, zother, yfar, 0), dr.at[11])
        for part in range(2):
            span = order[n] * 2 + part
            vt[span, :HD] = kv[1, span].T

    vt[:, HD:] = jnp.ones((16, 16, SPAN), bf16)

    score_scale = math.log2(math.e) / math.sqrt(HD)

    def fold(scores):
        return jnp.max(scores.reshape(SPAN // 8, 8, 256), axis=0)

    def scores_of(tile, key_span):
        keys = kv[0, key_span]
        keys = jnp.concatenate([keys, keys], axis=1)
        parts = [
            jnp.dot(keys[h * 256 : (h + 1) * 256], qt[tile], preferred_element_type=f32) for h in range(2)
        ]
        return jnp.concatenate(parts, axis=0)

    def start_of(span):
        row = posall[span // 2, pl.ds(pl.multiple_of((span % 2) * 8, 8), 8), :][0:1]
        return jnp.concatenate([row, row], axis=1)

    own_spans = (2 * ctx, 2 * ctx + 1)

    def attention(place, dests, during_gather):
        own_starts = [start_of(span) for span in own_spans]
        for tile in range(4):
            way, hh = tile // 2, tile % 2
            rows = qbuf[way * 4 + dests[way]]
            stack = jnp.concatenate(
                [rows[:, (hh * 4 + h) * HD : (hh * 4 + h + 1) * HD] for h in range(4)], axis=0
            )
            qf = stack.astype(f32).T * score_scale
            hi = qf.astype(bf16)
            lo = (qf - hi.astype(f32)).astype(bf16)
            qt[tile] = jnp.concatenate([hi, lo], axis=0)

        def masked(tile, s):
            key_at = lax.broadcasted_iota(jnp.int32, (SPAN, 256), 0)
            row_at = lax.broadcasted_iota(jnp.int32, (SPAN, 256), 1) % ROWS
            return jnp.where(key_at <= row_at + (dests[tile // 2] * 128 + core * ROWS), s, NEG)

        def span_at(tile, i):
            way = tile // 2
            if during_gather:
                return order[i // 2 % 8] * 2 + (i % 2 if way == 0 else 1 - i % 2)
            return (own_spans[way] + i) % 16

        def product(tile, i, slot):
            r = jnp.dot(vt[span_at(tile, i)], p_sc[slot], preferred_element_type=f32)[: HD + 8]
            acc[tile] = acc[tile] * a_sc[slot] + r

        def units(i, own):
            for tile in range(4):
                cur, nxt = tile % 2, (tile + 1) % 2
                after, ai = (tile + 1) % 4, i + (tile + 1) // 4
                before, bi = (tile + 3) % 4, i - (1 if tile == 0 else 0)
                last = during_gather and i == 15 and tile == 3
                top = jnp.max(t_sc[cur], axis=0, keepdims=True)
                old = m_sc[tile]
                if own:
                    new = offset = jnp.maximum(old, top)
                else:
                    visible = start_of(span_at(tile, i)) < own_starts[tile // 2]
                    bias = jnp.where(visible, 0.0, NEG).astype(f32)
                    new = jnp.maximum(old, top + bias)
                    offset = new - bias
                m_sc[tile] = new
                if not last:
                    s = scores_of(after, span_at(after, ai))
                    if own and tile < 3:
                        s = masked(after, s)
                if not (own and tile == 0):
                    product(before, bi, nxt)
                a_sc[cur] = jnp.exp2(old - new)
                tops = None
                for sub in range(4):
                    rows = slice(sub * 128, (sub + 1) * 128)
                    if not last:
                        s_sc[nxt, rows] = s[rows]
                        t = jnp.max(s[rows].reshape(16, 8, 256), axis=0)
                        tops = t if tops is None else jnp.maximum(tops, t)
                    p_sc[cur, rows] = jnp.exp2(s_sc[cur, rows] - offset).astype(bf16)
                if not last:
                    t_sc[nxt] = tops

        for tile in range(4):
            m_sc[tile] = jnp.full((1, 256), NEG, f32)
            acc[tile] = jnp.zeros((HD + 8, 256), f32)
        if during_gather:
            ready(0)
        s = masked(0, scores_of(0, own_spans[0]))
        s_sc[0] = s
        t_sc[0] = fold(s)
        if during_gather:
            gathered(1)
            units(0, True)
            for i in range(1, 8):
                src = posall.at[(ctx + 8 - i) % 8]
                rcopy(src, src, ps.at[0], pr.at[i - 1], mate).wait_recv()
            gathered(2)
            for n in range(8):
                if n in (2, 3, 5):
                    gathered({2: 4, 3: 5, 5: 7}[n])
                if n < 7:
                    ready(n + 1)
                for i in range(max(2 * n, 1), 2 * n + 2):
                    units(i, False)
        else:
            units(0, True)

            @pl.loop(1, 16)
            def _(i):
                units(i, False)

        product(3, 15, 1)

        for tile in range(4):
            way, hh = tile // 2, tile % 2
            out = (acc[tile, :HD] / acc[tile, HD : HD + 1]).T.astype(bf16)
            for h in range(4):
                head = hh * 4 + h
                att[place, way * ROWS : (way + 1) * ROWS, head * HD : (head + 1) * HD] = out[
                    h * ROWS : (h + 1) * ROWS
                ]

    def projected(place, cols):
        r = jnp.dot(att[place, :, :512], wbuf[0, :, cols], preferred_element_type=f32)
        return r + jnp.dot(att[place, :, 512:], wbuf[1, :, cols], preferred_element_type=f32)

    mine = zhi == 0

    def across(step, place):
        for chunk in range(A_CHUNKS):
            piece = pl.ds(chunk * A_PER, A_PER)
            if step == 0:
                weights_here(chunk)
            if step > 0:
                for way in range(2):
                    arrived(recv.at[way, step - 1, :, piece], xr.at[way, step - 1, chunk])

            @pl.loop(0, A_PER // TILE)
            def _(t):
                cols = pl.ds(pl.multiple_of(chunk * A_PER + t * TILE, TILE), TILE)
                r = projected(place, cols)
                up, down = r[:ROWS], r[ROWS:]
                if step > 0:
                    up += recv[0, step - 1, :, cols].astype(f32)
                    down += recv[1, step - 1, :, cols].astype(f32)
                if step < 3:
                    send[0, step, :, cols] = up.astype(bf16)
                    send[1, step, :, cols] = down.astype(bf16)
                else:
                    summed[:, cols] = jnp.where(mine, up, down)
                    fin[:, cols] = jnp.where(mine, down, up).astype(bf16)

            if step < 3:
                for way, dev in ((0, xup), (1, xdn)):
                    start(
                        rcopy(
                            send.at[way, step, :, piece], recv.at[way, step, :, piece],
                            xs.at[way, step, chunk], xr.at[way, step, chunk], dev,
                        )
                    )
            else:
                start(rcopy(fin.at[:, piece], zrecv.at[:, piece], zs.at[chunk], zr.at[chunk], zmate))

    def begin(ring, step, place):
        weights_here(*((5, 6) if ring == 0 else (6, 7)))

        @pl.loop(0, B_COLS // TILE)
        def _(t):
            cols = pl.ds(pl.multiple_of(t * TILE, TILE), TILE)
            r = projected(
                place, pl.ds(pl.multiple_of(A_COLS + ring * B_COLS + t * TILE, TILE), TILE)
            )
            bown[ring, step, :, cols] = jnp.where(mine, r[:ROWS], r[ROWS:])
            zsend[ring, step, :, cols] = jnp.where(mine, r[ROWS:], r[:ROWS]).astype(bf16)

        start(
            rcopy(
                zsend.at[ring, step], zgot.at[ring, step], bzs.at[ring, step], bzr.at[ring, step], zmate
            )
        )

    def finish(ring, step):
        arrived(zgot.at[ring, step], bzr.at[ring, step])
        if step > 0:
            arrived(brecv.at[ring, step - 1], bxr.at[ring, step - 1])

        @pl.loop(0, B_COLS // TILE)
        def _(t):
            cols = pl.ds(pl.multiple_of(t * TILE, TILE), TILE)
            v = bown[ring, step, :, cols] + zgot[ring, step, :, cols].astype(f32)
            if step > 0:
                v += brecv[ring, step - 1, :, cols].astype(f32)
            if step < 3:
                bsend[ring, step, :, cols] = v.astype(bf16)
            else:
                summed[:, pl.ds(pl.multiple_of(A_COLS + ring * B_COLS + t * TILE, TILE), TILE)] = v

        if step < 3:
            ahead = (x + jnp.where((zhi + ring) % 2 == 0, 1, 3)) % 4
            start(
                rcopy(
                    bsend.at[ring, step], brecv.at[ring, step], bxs.at[ring, step], bxr.at[ring, step],
                    at_tp(zhi, ahead, core),
                )
            )

    left, right, far = (x + 3) % 4, (x + 1) % 4, (x + 2) % 4
    loads[5].wait()
    qother = qbuf.at[:, :, pl.ds(pl.multiple_of((1 - core) * 512, 512), 512)]
    arrived(qother, qsem.at[1])
    attention(0, (left, right), True)
    weights_on(8)
    loads[6].wait()
    begin(0, 0, 0)
    across(0, 0)
    begin(1, 2, 0)
    attention(1, (far, far), False)
    finish(0, 0)
    begin(0, 1, 1)
    begin(1, 1, 1)
    across(1, 1)
    attention(2, (right, left), False)
    begin(1, 0, 2)
    begin(0, 2, 2)
    finish(0, 1)
    finish(1, 0)
    across(2, 2)
    attention(3, (x, x), False)
    begin(0, 3, 3)
    begin(1, 3, 3)
    finish(0, 2)
    finish(1, 1)
    across(3, 3)
    finish(0, 3)
    finish(1, 2)
    finish(1, 3)

    loads[7].wait()
    loads[8].wait()
    squares = jnp.zeros((ROWS, TILE), f32)

    def total_of(start_col, crossed):
        cols = slice(start_col, start_col + TILE)
        total = summed[:, cols] + res[:, cols].astype(f32)
        if crossed:
            total += zrecv[:, cols].astype(f32)
        summed[:, cols] = total
        hidden_ref[:, cols] = total.astype(bf16)
        return total * total

    for t in range(A_COLS, WIDTH, TILE):
        squares += total_of(t, False)
    for chunk in range(A_CHUNKS):
        arrived(zrecv.at[:, pl.ds(chunk * A_PER, A_PER)], zr.at[chunk])
        for t in range(chunk * A_PER, (chunk + 1) * A_PER, TILE):
            squares += total_of(t, True)
    inv_rms = lax.rsqrt(jnp.sum(squares, axis=1, keepdims=True) * (1.0 / WIDTH) + 1e-5)
    limit = 448.0 * scale_ref[0]
    for t in range(WIDTH // TILE):
        cols = slice(t * TILE, (t + 1) * TILE)
        value = summed[:, cols] * inv_rms * gain[:, cols]
        clipped_ref[:, cols] = jnp.minimum(jnp.maximum(value, -limit), limit).astype(bf16)
    for copy in started:
        copy.wait_send()


def shards(queries, context_keys, context_values, positions, out_weight, residual_in, norm_gain, static_scale):
    starts = jnp.broadcast_to(positions.reshape(2, SPAN)[:, :1, None], (2, 8, 128)).reshape(16, 128)
    dma = pltpu.SemaphoreType.DMA
    out = jax.ShapeDtypeStruct((ROWS, WIDTH), bf16)
    anywhere = pl.BlockSpec(memory_space=pl.ANY)
    return pl.pallas_call(
        kernel,
        out_shape=(out, out),
        in_specs=[anywhere] * 7 + [pl.BlockSpec(memory_space=pltpu.SMEM)],
        out_specs=(pl.BlockSpec(memory_space=pltpu.VMEM),) * 2,
        scratch_shapes=[
            pltpu.VMEM((2, 512, WIDTH), bf16),
            pltpu.VMEM((2, 16, SPAN, HD), bf16),
            pltpu.VMEM((2, 1, SPAN, HD), bf16),
            pltpu.VMEM((16, HD + 16, SPAN), bf16),
            pltpu.VMEM((8, ROWS, 1024), bf16),
            pltpu.VMEM((8, 16, 128), jnp.int32),
            pltpu.VMEM((4, 2 * HD, 256), bf16),
            pltpu.VMEM((4, HD + 8, 256), f32),
            pltpu.VMEM((4, 1, 256), f32),
            pltpu.VMEM((2, 1, 256), f32),
            pltpu.VMEM((2, 8, 256), f32),
            pltpu.VMEM((2, SPAN, 256), f32),
            pltpu.VMEM((2, SPAN, 256), bf16),
            pltpu.VMEM((4, 2 * ROWS, 1024), bf16),
            pltpu.VMEM((2, 3, ROWS, A_COLS), bf16),
            pltpu.VMEM((2, 3, ROWS, A_COLS), bf16),
            pltpu.VMEM((2, 4, ROWS, B_COLS), bf16),
            pltpu.VMEM((2, 4, ROWS, B_COLS), bf16),
            pltpu.VMEM((2, 4, ROWS, B_COLS), f32),
            pltpu.VMEM((2, 3, ROWS, B_COLS), bf16),
            pltpu.VMEM((2, 3, ROWS, B_COLS), bf16),
            pltpu.VMEM((ROWS, A_COLS), bf16),
            pltpu.VMEM((ROWS, A_COLS), bf16),
            pltpu.VMEM((ROWS, WIDTH), f32),
            pltpu.VMEM((ROWS, WIDTH), bf16),
            pltpu.VMEM((1, WIDTH), f32),
            dma((9,)), dma((2,)), dma((2, 8)), dma((12,)), dma((12,)), dma((12,)), dma((12,)), dma((7,)), dma((7,)),
            dma((2, 3, A_CHUNKS)), dma((2, 3, A_CHUNKS)), dma((2, 4)), dma((2, 4)), dma((2, 3)), dma((2, 3)),
            dma((A_CHUNKS,)), dma((A_CHUNKS,)),
        ],
        compiler_params=pltpu.CompilerParams(
            collective_id=0, has_side_effects=True, vmem_limit_bytes=62 * 1024 * 1024
        ),
    )(
        queries.reshape(8, 2, ROWS, 512),
        context_keys.reshape(2, SPAN, 1024),
        context_values.reshape(2, SPAN, 1024),
        starts,
        out_weight,
        residual_in,
        norm_gain.reshape(1, WIDTH),
        static_scale,
    )


def solution(mesh):
    return jax.shard_map(
        shards,
        mesh=mesh,
        in_specs=(
            P("ctx", "tp"),
            P("ctx", None),
            P("ctx", None),
            P("ctx"),
            P("tp", None),
            P(("ctx", "tp"), None),
            P(),
            P(),
        ),
        out_specs=(P(("ctx", "tp"), None), P(("ctx", "tp"), None)),
        check_vma=False,
    )
```

time: 189 us -> 121 us (0.64)
  Pallas kernels: 183 us -> 114 us
    pallas_call x1, Pallas kernels: 183 us -> 114 us  [shards(): pl.pallas_call(kernel, out_shape=(out, out), in_specs=[anywhere] * 7 + [p...]
where the time goes in v2:
time: 121 us; the launch traced here: 120 us
  Pallas kernels  114 us (94%)
  local copies, waits for them, and re-layouts  4.97 us (4%)
  between operations  1.3 us (1%)
    pallas_call x1, Pallas kernels, shards(): pl.pallas_call(kernel, out_shape=(out, out), in_specs=[anywhere] * 7 + [p...  114 us
    unnamed x4, local copies, waits for them, and re-layouts  3.32 us

profile of v2, /device:TPU:1, one launch (start us, length us, event | category | flops | bytes accessed | tf_op | source)
XLA Modules:
  0.0 120.4 jit_solution(2105596519299147611)
XLA Ops:
  1.3 0.7 reshape.25
  2.0 0.1 slice_reduce_fusion
  2.1 0.1 broadcast_in_dim.13
  2.2 0.1 broadcast_in_dim.14
  2.2 0.7 broadcast_in_dim.15.pos_hbm
  2.9 114.2 %shard_map.95 = (bf16[64,8192]{1,0:T(8,128)(2,1)}, bf16[64,8192]{1,0:T(8,128)(2,1)}) custom-call(bf16[8,2,64,512]{3,2,1,0:T(8,128)(2,1)} %bitcast.6, bf16[2,512,1024]{2,1,0:T(8,128)(2,1)} %bitcast.4, bf16[2,512,1024]{2,1,0:T(8,128)(2,1)} %bitcast.5, s32[16,128]{1,0:T(8,128)} %broadcast_in_dim.15.pos_hbm, bf16[512,8192]{1,0:T(8,128)(2,1)} %w_hbm.1, ...), custom_call_target="tpu_custom_call" | custom-call | tf_op jit(solution)/shard_map/pallas_call | solution.py:496
  117.1 0.0 copy-start
  117.1 2.4 %copy.13 = bf16[64,8192]{1,0:T(8,128)(2,1)} copy(bf16[64,8192]{1,0:T(8,128)(2,1)} %get-tuple-element.4) | data formatting | bytes 2097152
  119.4 0.0 copy-done
  119.4 1.0 copy.14
Async XLA Ops:
  117.1 2.4 %copy-start = (bf16[64,8192]{1,0:T(8,128)(2,1)S(1)}, bf16[64,8192]{1,0:T(8,128)(2,1)}, u32[]{:S(2)}) copy-start(bf16[64,8192]{1,0:T(8,128)(2,1)} %get-tuple-element.5) | copy-start | bytes 3145732

commit v3 on v2

--- a/solution.py
+++ b/solution.py
@@ -12,6 +12,9 @@
 ROWS = 64
 WIDTH = 8192
 TILE = 512
+NORM_ROWS = 16
+A_TILE = 1024
+B_TILE = 1536
 A_COLS = 5120
 A_CHUNKS = 5
 A_PER = A_COLS // A_CHUNKS
@@ -23,11 +26,11 @@
 
 
 def kernel(
-    q_hbm, k_hbm, v_hbm, pos_hbm, w_hbm, res_hbm, gain_hbm, scale_ref,
-    hidden_ref, clipped_ref,
+    q_hbm, k_hbm, v_hbm, pos_hbm, w_hbm, res_hbm,
+    total_hbm,
     wbuf, kv, foreign, vt, qbuf, posall, qt, acc, m_sc, a_sc, t_sc, s_sc, p_sc, att,
-    send, recv, zsend, zgot, bown, bsend, brecv, fin, zrecv, summed, res, gain,
-    lsem, qsem, wsem, gs, gr, ds, dr, ps, pr, xs, xr, bzs, bzr, bxs, bxr, zs, zr,
+    send, recv, zsend, zgot, bown, bsend, brecv, fin, zrecv, summed, res,
+    lsem, tsem, qsem, wsem, gs, gr, ds, dr, ps, pr, xs, xr, bzs, bzr, bxs, bxr, zs, zr,
 ):
     ctx = lax.axis_index("ctx")
     tp = lax.axis_index("tp")
@@ -70,7 +73,6 @@
         (q_hbm.at[:, core], qbuf.at[:, :, qcol]),
         (w_hbm, wbuf.at[core]),
         (res_hbm, res),
-        (gain_hbm, gain),
     )):
         copy = pltpu.make_async_copy(source, target, lsem.at[n])
         copy.start()
@@ -120,6 +122,9 @@
     def pass_on(ref, n):
         start(rcopy(ref, ref, ds.at[n], dr.at[n], mate))
 
+    loads[4].wait()
+    for i in range(1, 8):
+        start(rcopy(posall.at[ctx], posall.at[ctx], ps.at[i - 1], pr.at[i - 1], ((ctx + i) % 8, tp)))
     for n in range(4):
         loads[n].wait()
     first = half(core, zlo, y, 0)
@@ -129,9 +134,6 @@
     send_on(own, 2, yabove)
     send_on(own, 3, ybelow)
     start(rcopy(q_hbm.at[:, 1 - core], qbuf.at[:, :, qcol], qsem.at[0], qsem.at[1], mate))
-    loads[4].wait()
-    for i in range(1, 8):
-        start(rcopy(posall.at[ctx], posall.at[ctx], ps.at[i - 1], pr.at[i - 1], ((ctx + i) % 8, tp)))
     weights_on(2)
 
     order = [
@@ -228,116 +230,152 @@
     def fold(scores):
         return jnp.max(scores.reshape(SPAN // 8, 8, 256), axis=0)
 
-    def scores_of(tile, key_span):
+    def scores_of(place, tile, key_span):
         keys = kv[0, key_span]
         keys = jnp.concatenate([keys, keys], axis=1)
         parts = [
-            jnp.dot(keys[h * 256 : (h + 1) * 256], qt[tile], preferred_element_type=f32) for h in range(2)
+            jnp.dot(keys[h * 256 : (h + 1) * 256], qt[place, tile], preferred_element_type=f32) for h in range(2)
         ]
         return jnp.concatenate(parts, axis=0)
 
     def start_of(span):
-        row = posall[span // 2, pl.ds(pl.multiple_of((span % 2) * 8, 8), 8), :][0:1]
+        row = posall[span // 2, pl.ds((span % 2) * (SPAN // 128), 1), :]
         return jnp.concatenate([row, row], axis=1)
 
     own_spans = (2 * ctx, 2 * ctx + 1)
 
-    def attention(place, dests, during_gather):
-        own_starts = [start_of(span) for span in own_spans]
+    def prepare(place):
         for tile in range(4):
             way, hh = tile // 2, tile % 2
-            rows = qbuf[way * 4 + dests[way]]
+            rows = qbuf[way * 4 + visits[place][way]]
             stack = jnp.concatenate(
                 [rows[:, (hh * 4 + h) * HD : (hh * 4 + h + 1) * HD] for h in range(4)], axis=0
             )
             qf = stack.astype(f32).T * score_scale
             hi = qf.astype(bf16)
             lo = (qf - hi.astype(f32)).astype(bf16)
-            qt[tile] = jnp.concatenate([hi, lo], axis=0)
-
-        def masked(tile, s):
-            key_at = lax.broadcasted_iota(jnp.int32, (SPAN, 256), 0)
-            row_at = lax.broadcasted_iota(jnp.int32, (SPAN, 256), 1) % ROWS
-            return jnp.where(key_at <= row_at + (dests[tile // 2] * 128 + core * ROWS), s, NEG)
-
-        def span_at(tile, i):
-            way = tile // 2
-            if during_gather:
-                return order[i // 2 % 8] * 2 + (i % 2 if way == 0 else 1 - i % 2)
-            return (own_spans[way] + i) % 16
-
-        def product(tile, i, slot):
-            r = jnp.dot(vt[span_at(tile, i)], p_sc[slot], preferred_element_type=f32)[: HD + 8]
-            acc[tile] = acc[tile] * a_sc[slot] + r
-
-        def units(i, own):
-            for tile in range(4):
-                cur, nxt = tile % 2, (tile + 1) % 2
-                after, ai = (tile + 1) % 4, i + (tile + 1) // 4
-                before, bi = (tile + 3) % 4, i - (1 if tile == 0 else 0)
-                last = during_gather and i == 15 and tile == 3
-                top = jnp.max(t_sc[cur], axis=0, keepdims=True)
-                old = m_sc[tile]
-                if own:
-                    new = offset = jnp.maximum(old, top)
-                else:
-                    visible = start_of(span_at(tile, i)) < own_starts[tile // 2]
-                    bias = jnp.where(visible, 0.0, NEG).astype(f32)
-                    new = jnp.maximum(old, top + bias)
-                    offset = new - bias
-                m_sc[tile] = new
-                if not last:
-                    s = scores_of(after, span_at(after, ai))
-                    if own and tile < 3:
-                        s = masked(after, s)
-                if not (own and tile == 0):
-                    product(before, bi, nxt)
-                a_sc[cur] = jnp.exp2(old - new)
-                tops = None
-                for sub in range(4):
-                    rows = slice(sub * 128, (sub + 1) * 128)
-                    if not last:
-                        s_sc[nxt, rows] = s[rows]
-                        t = jnp.max(s[rows].reshape(16, 8, 256), axis=0)
-                        tops = t if tops is None else jnp.maximum(tops, t)
-                    p_sc[cur, rows] = jnp.exp2(s_sc[cur, rows] - offset).astype(bf16)
-                if not last:
-                    t_sc[nxt] = tops
-
-        for tile in range(4):
-            m_sc[tile] = jnp.full((1, 256), NEG, f32)
-            acc[tile] = jnp.zeros((HD + 8, 256), f32)
-        if during_gather:
-            ready(0)
-        s = masked(0, scores_of(0, own_spans[0]))
+            qt[place, tile] = jnp.concatenate([hi, lo], axis=0)
+
+    left, right, far = (x + 3) % 4, (x + 1) % 4, (x + 2) % 4
+    visits = ((left, right), (far, far), (right, left), (x, x))
+
+    own_starts = [start_of(span) for span in own_spans]
+
+    def own_span(tile, i):
+        way = tile // 2
+        return 2 * ctx + (way if i == 0 else 1 - way)
+
+    def arriving_span(tile, i):
+        return order[i // 2 % 8] * 2 + i % 2
+
+    def other_span(tile, i):
+        return (2 * ctx + i) % 16
+
+    def masked(place, tile, s):
+        key_at = lax.broadcasted_iota(jnp.int32, (SPAN, 256), 0)
+        row_at = lax.broadcasted_iota(jnp.int32, (SPAN, 256), 1) % ROWS
+        return jnp.where(key_at <= row_at + (visits[place][tile // 2] * 128 + core * ROWS), s, NEG)
+
+    def product(place, tile, span, slot):
+        r = jnp.dot(vt[span], p_sc[slot], preferred_element_type=f32)[: HD + 8]
+        acc[place, tile] = acc[place, tile] * a_sc[slot] + r
+
+    def opening(place, span, own=False):
+        s = scores_of(place, 0, span)
+        if own:
+            s = masked(place, 0, s)
         s_sc[0] = s
         t_sc[0] = fold(s)
-        if during_gather:
-            gathered(1)
-            units(0, True)
-            for i in range(1, 8):
-                src = posall.at[(ctx + 8 - i) % 8]
-                rcopy(src, src, ps.at[0], pr.at[i - 1], mate).wait_recv()
-            gathered(2)
-            for n in range(8):
-                if n in (2, 3, 5):
-                    gathered({2: 4, 3: 5, 5: 7}[n])
-                if n < 7:
-                    ready(n + 1)
-                for i in range(max(2 * n, 1), 2 * n + 2):
-                    units(i, False)
-        else:
-            units(0, True)
-
-            @pl.loop(1, 16)
-            def _(i):
-                units(i, False)
-
-        product(3, 15, 1)
-
+
+    def units(place, span_at, i, own=False, first=False, last=False):
+        for tile in range(4):
+            cur, nxt = tile % 2, (tile + 1) % 2
+            after, ai = (tile + 1) % 4, i + (tile + 1) // 4
+            before, bi = (tile + 3) % 4, i - (1 if tile == 0 else 0)
+            ends = last and tile == 3
+            top = jnp.max(t_sc[cur], axis=0, keepdims=True)
+            old = m_sc[place, tile]
+            if own:
+                new = offset = jnp.maximum(old, top)
+            else:
+                visible = start_of(span_at(tile, i)) < own_starts[tile // 2]
+                bias = jnp.where(visible, 0.0, NEG).astype(f32)
+                new = jnp.maximum(old, top + bias)
+                offset = new - bias
+            m_sc[place, tile] = new
+            if not ends:
+                s = scores_of(place, after, span_at(after, ai))
+                if own and tile < 3:
+                    s = masked(place, after, s)
+            if not (first and tile == 0):
+                product(place, before, span_at(before, bi), nxt)
+            a_sc[cur] = jnp.exp2(old - new)
+            tops = None
+            for sub in range(4):
+                rows = slice(sub * 128, (sub + 1) * 128)
+                if not ends:
+                    s_sc[nxt, rows] = s[rows]
+                    t = jnp.max(s[rows].reshape(16, 8, 256), axis=0)
+                    tops = t if tops is None else jnp.maximum(tops, t)
+                p_sc[cur, rows] = jnp.exp2(s_sc[cur, rows] - offset).astype(bf16)
+            if not ends:
+                t_sc[nxt] = tops
+
+    def attend_own(place):
+        prepare(place)
+        for tile in range(4):
+            m_sc[place, tile] = jnp.full((1, 256), NEG, f32)
+            acc[place, tile] = jnp.zeros((HD + 8, 256), f32)
+        opening(place, own_span(0, 0), True)
+        units(place, own_span, 0, own=True, first=True)
+        units(place, own_span, 1, last=True)
+        product(place, 3, own_span(3, 1), 1)
+
+    def attend_arriving():
+        ready(0)
+        attend_own(0)
+        attend_own(1)
+        gathered(1)
+        attend_own(2)
+        for i in range(1, 8):
+            src = posall.at[(ctx + 8 - i) % 8]
+            rcopy(src, src, ps.at[0], pr.at[i - 1], mate).wait_recv()
+        gathered(2)
+        attend_own(3)
+        ready(1)
+        opening(0, arriving_span(0, 2))
+        for n in range(1, 8):
+            if n in (2, 3, 5):
+                gathered({2: 4, 3: 5, 5: 7}[n])
+            if n < 7:
+                ready(n + 1)
+            units(0, arriving_span, 2 * n, first=n == 1)
+            units(0, arriving_span, 2 * n + 1, last=n == 7)
+        product(0, 3, arriving_span(3, 15), 1)
+        attended(0)
+
+    def attend_others(place, between=None):
+        opening(place, other_span(0, 2))
+        p_sc[1] = jnp.zeros((SPAN, 256), bf16)
+        a_sc[1] = jnp.ones((1, 256), f32)
+
+        for low, high in ((1, 8),) if between is None else ((1, 4), (4, 8)):
+
+            @pl.loop(low, high)
+            def _(n):
+                units(place, other_span, 2 * n)
+                units(place, other_span, 2 * n + 1)
+
+            if high == 4:
+                between()
+
+        product(place, 3, other_span(3, 15), 1)
+        attended(place)
+
+    def attended(place):
         for tile in range(4):
             way, hh = tile // 2, tile % 2
-            out = (acc[tile, :HD] / acc[tile, HD : HD + 1]).T.astype(bf16)
+            out = (acc[place, tile, :HD] / acc[place, tile, HD : HD + 1]).T.astype(bf16)
             for h in range(4):
                 head = hh * 4 + h
                 att[place, way * ROWS : (way + 1) * ROWS, head * HD : (head + 1) * HD] = out[
@@ -350,8 +388,8 @@
 
     mine = zhi == 0
 
-    def across(step, place):
-        for chunk in range(A_CHUNKS):
+    def across(step, place, chunks=range(A_CHUNKS)):
+        for chunk in chunks:
             piece = pl.ds(chunk * A_PER, A_PER)
             if step == 0:
                 weights_here(chunk)
@@ -359,9 +397,8 @@
                 for way in range(2):
                     arrived(recv.at[way, step - 1, :, piece], xr.at[way, step - 1, chunk])
 
-            @pl.loop(0, A_PER // TILE)
-            def _(t):
-                cols = pl.ds(pl.multiple_of(chunk * A_PER + t * TILE, TILE), TILE)
+            for t in range(A_PER // A_TILE):
+                cols = pl.ds(chunk * A_PER + t * A_TILE, A_TILE)
                 r = projected(place, cols)
                 up, down = r[:ROWS], r[ROWS:]
                 if step > 0:
@@ -388,12 +425,9 @@
     def begin(ring, step, place):
         weights_here(*((5, 6) if ring == 0 else (6, 7)))
 
-        @pl.loop(0, B_COLS // TILE)
-        def _(t):
-            cols = pl.ds(pl.multiple_of(t * TILE, TILE), TILE)
-            r = projected(
-                place, pl.ds(pl.multiple_of(A_COLS + ring * B_COLS + t * TILE, TILE), TILE)
-            )
+        for t in range(B_COLS // B_TILE):
+            cols = pl.ds(t * B_TILE, B_TILE)
+            r = projected(place, pl.ds(A_COLS + ring * B_COLS + t * B_TILE, B_TILE))
             bown[ring, step, :, cols] = jnp.where(mine, r[:ROWS], r[ROWS:])
             zsend[ring, step, :, cols] = jnp.where(mine, r[ROWS:], r[:ROWS]).astype(bf16)
 
@@ -428,86 +462,100 @@
                 )
             )
 
-    left, right, far = (x + 3) % 4, (x + 1) % 4, (x + 2) % 4
     loads[5].wait()
     qother = qbuf.at[:, :, pl.ds(pl.multiple_of((1 - core) * 512, 512), 512)]
     arrived(qother, qsem.at[1])
-    attention(0, (left, right), True)
+    attend_arriving()
     weights_on(8)
     loads[6].wait()
     begin(0, 0, 0)
     across(0, 0)
     begin(1, 2, 0)
-    attention(1, (far, far), False)
+    attend_others(1)
     finish(0, 0)
     begin(0, 1, 1)
     begin(1, 1, 1)
-    across(1, 1)
-    attention(2, (right, left), False)
+    across(1, 1, range(2))
+    attend_others(2, lambda: across(1, 1, range(2, A_CHUNKS)))
     begin(1, 0, 2)
     begin(0, 2, 2)
     finish(0, 1)
-    finish(1, 0)
-    across(2, 2)
-    attention(3, (x, x), False)
+
+    def meanwhile():
+        across(2, 2, range(3))
+        finish(1, 0)
+
+    attend_others(3, meanwhile)
     begin(0, 3, 3)
     begin(1, 3, 3)
     finish(0, 2)
     finish(1, 1)
-    across(3, 3)
+    across(2, 2, range(3, A_CHUNKS))
+    across(3, 3, range(3))
+    finish(1, 2)
+    across(3, 3, range(3, A_CHUNKS))
     finish(0, 3)
-    finish(1, 2)
     finish(1, 3)
 
     loads[7].wait()
-    loads[8].wait()
-    squares = jnp.zeros((ROWS, TILE), f32)
-
-    def total_of(start_col, crossed):
-        cols = slice(start_col, start_col + TILE)
-        total = summed[:, cols] + res[:, cols].astype(f32)
-        if crossed:
-            total += zrecv[:, cols].astype(f32)
-        summed[:, cols] = total
-        hidden_ref[:, cols] = total.astype(bf16)
-        return total * total
-
-    for t in range(A_COLS, WIDTH, TILE):
-        squares += total_of(t, False)
+    stores = []
+
+    def hand_out(n, low, high, crossed):
+        for t in range(low, high, TILE):
+            cols = slice(t, t + TILE)
+            total = summed[:, cols] + res[:, cols].astype(f32)
+            if crossed:
+                total += zrecv[:, cols].astype(f32)
+            summed[:, cols] = total
+        piece = pl.ds(low, high - low)
+        copy = pltpu.make_async_copy(summed.at[:, piece], total_hbm.at[:, piece], tsem.at[n])
+        copy.start()
+        stores.append(copy)
+
+    hand_out(A_CHUNKS, A_COLS, WIDTH, False)
     for chunk in range(A_CHUNKS):
         arrived(zrecv.at[:, pl.ds(chunk * A_PER, A_PER)], zr.at[chunk])
-        for t in range(chunk * A_PER, (chunk + 1) * A_PER, TILE):
-            squares += total_of(t, True)
+        hand_out(chunk, chunk * A_PER, (chunk + 1) * A_PER, True)
+    for copy in stores:
+        copy.wait()
+    for copy in started:
+        copy.wait_send()
+
+
+def norm_kernel(scale_ref, total_ref, gain_ref, hidden_ref, clipped_ref):
+    squares = jnp.zeros((NORM_ROWS, TILE), f32)
+    for t in range(0, WIDTH, TILE):
+        total = total_ref[:, t : t + TILE]
+        hidden_ref[:, t : t + TILE] = total.astype(bf16)
+        squares += total * total
     inv_rms = lax.rsqrt(jnp.sum(squares, axis=1, keepdims=True) * (1.0 / WIDTH) + 1e-5)
     limit = 448.0 * scale_ref[0]
+    per = TILE // 128
     for t in range(WIDTH // TILE):
         cols = slice(t * TILE, (t + 1) * TILE)
-        value = summed[:, cols] * inv_rms * gain[:, cols]
+        gain = jnp.concatenate([gain_ref[t * per + i : t * per + i + 1, :] for i in range(per)], axis=1)
+        value = total_ref[:, cols] * inv_rms * gain
         clipped_ref[:, cols] = jnp.minimum(jnp.maximum(value, -limit), limit).astype(bf16)
-    for copy in started:
-        copy.wait_send()
 
 
 def shards(queries, context_keys, context_values, positions, out_weight, residual_in, norm_gain, static_scale):
-    starts = jnp.broadcast_to(positions.reshape(2, SPAN)[:, :1, None], (2, 8, 128)).reshape(16, 128)
     dma = pltpu.SemaphoreType.DMA
-    out = jax.ShapeDtypeStruct((ROWS, WIDTH), bf16)
     anywhere = pl.BlockSpec(memory_space=pl.ANY)
-    return pl.pallas_call(
+    total = pl.pallas_call(
         kernel,
-        out_shape=(out, out),
-        in_specs=[anywhere] * 7 + [pl.BlockSpec(memory_space=pltpu.SMEM)],
-        out_specs=(pl.BlockSpec(memory_space=pltpu.VMEM),) * 2,
+        out_shape=jax.ShapeDtypeStruct((ROWS, WIDTH), f32),
+        in_specs=[anywhere] * 6,
+        out_specs=anywhere,
         scratch_shapes=[
             pltpu.VMEM((2, 512, WIDTH), bf16),
             pltpu.VMEM((2, 16, SPAN, HD), bf16),
             pltpu.VMEM((2, 1, SPAN, HD), bf16),
             pltpu.VMEM((16, HD + 16, SPAN), bf16),
             pltpu.VMEM((8, ROWS, 1024), bf16),
-            pltpu.VMEM((8, 16, 128), jnp.int32),
-            pltpu.VMEM((4, 2 * HD, 256), bf16),
-            pltpu.VMEM((4, HD + 8, 256), f32),
-            pltpu.VMEM((4, 1, 256), f32),
+            pltpu.VMEM((8, 8, 128), jnp.int32),
+            pltpu.VMEM((4, 4, 2 * HD, 256), bf16),
+            pltpu.VMEM((4, 4, HD + 8, 256), f32),
+            pltpu.VMEM((4, 4, 1, 256), f32),
             pltpu.VMEM((2, 1, 256), f32),
             pltpu.VMEM((2, 8, 256), f32),
             pltpu.VMEM((2, SPAN, 256), f32),
@@ -524,8 +572,7 @@
             pltpu.VMEM((ROWS, A_COLS), bf16),
             pltpu.VMEM((ROWS, WIDTH), f32),
             pltpu.VMEM((ROWS, WIDTH), bf16),
-            pltpu.VMEM((1, WIDTH), f32),
-            dma((9,)), dma((2,)), dma((2, 8)), dma((12,)), dma((12,)), dma((12,)), dma((12,)), dma((7,)), dma((7,)),
+            dma((8,)), dma((A_CHUNKS + 1,)), dma((2,)), dma((2, 8)), dma((12,)), dma((12,)), dma((12,)), dma((12,)), dma((7,)), dma((7,)),
             dma((2, 3, A_CHUNKS)), dma((2, 3, A_CHUNKS)), dma((2, 4)), dma((2, 4)), dma((2, 3)), dma((2, 3)),
             dma((A_CHUNKS,)), dma((A_CHUNKS,)),
         ],
@@ -536,12 +583,23 @@
         queries.reshape(8, 2, ROWS, 512),
         context_keys.reshape(2, SPAN, 1024),
         context_values.reshape(2, SPAN, 1024),
-        starts,
+        positions.reshape(8, 128),
         out_weight,
         residual_in,
-        norm_gain.reshape(1, WIDTH),
-        static_scale,
     )
+    out = jax.ShapeDtypeStruct((ROWS, WIDTH), bf16)
+    rows = pl.BlockSpec((NORM_ROWS, WIDTH), lambda i: (i, 0))
+    return pl.pallas_call(
+        norm_kernel,
+        grid=(ROWS // NORM_ROWS,),
+        out_shape=(out, out),
+        in_specs=[
+            pl.BlockSpec(memory_space=pltpu.SMEM),
+            rows,
+            pl.BlockSpec((WIDTH // 128, 128), lambda i: (0, 0)),
+        ],
+        out_specs=(rows, rows),
+    )(static_scale, total, norm_gain.reshape(WIDTH // 128, 128))
 
 
 def solution(mesh):

time: 121 us -> 103 us (0.85)
  Pallas kernels: 114 us -> 101 us
  local copies, waits for them, and re-layouts: 4.97 us -> 0 us
    pallas_call x1 -> x2, Pallas kernels: 114 us -> 101 us  [the longest x1 97.5 us: shards(): pl.pallas_call(kernel, out_shape=jax.ShapeDtypeStruct((ROWS, WIDTH), f32)...]
    unnamed x4 -> x0, local copies, waits for them, and re-layouts: 3.32 us -> none
where the time goes in v3:
time: 103 us
  Pallas kernels  101 us (98%)
  between operations  1.29 us (1%)
    pallas_call x1, Pallas kernels, shards(): pl.pallas_call(kernel, out_shape=jax.ShapeDtypeStruct((ROWS, WIDTH), f32)...  97.5 us
    pallas_call x1, Pallas kernels, shards(): pl.pallas_call(norm_kernel, grid=(ROWS // NORM_ROWS,), out_shape=(out, ou...  3.92 us

profile of v3, /device:TPU:1, one launch (start us, length us, event | category | flops | bytes accessed | tf_op | source)
XLA Modules:
  0.0 102.7 jit_solution(18039779292822041029)
XLA Ops:
  1.3 97.5 %shard_map.95.total_ref = f32[64,8192]{1,0:T(8,128)} custom-call(bf16[8,2,64,512]{3,2,1,0:T(8,128)(2,1)} %bitcast.7, bf16[2,512,1024]{2,1,0:T(8,128)(2,1)} %bitcast.5, bf16[2,512,1024]{2,1,0:T(8,128)(2,1)} %bitcast.6, s32[8,128]{1,0:T(8,128)} %bitcast.9, bf16[512,8192]{1,0:T(8,128)(2,1)} %w_hbm.1, bf16[64,8192]{1,0:T(8,128)(2,1)} %res_hbm.1), custom_call_target="tpu_custom_call" | custom-call | tf_op jit(solution)/shard_map/pallas_call | solution.py:544
  98.7 3.9 %shard_map.96 = (bf16[64,8192]{1,0:T(8,128)(2,1)}, bf16[64,8192]{1,0:T(8,128)(2,1)}) custom-call(f32[1]{0:T(128)S(6)} %copy.10.scale_ref, f32[64,8192]{1,0:T(8,128)} %shard_map.95.total_ref, f32[64,128]{1,0:T(8,128)} %bitcast.8), custom_call_target="tpu_custom_call" | custom-call | tf_op jit(solution)/shard_map/pallas_call | solution.py:592

commit v4 on v3

--- a/solution.py
+++ b/solution.py
@@ -12,12 +12,13 @@
 ROWS = 64
 WIDTH = 8192
 TILE = 512
-NORM_ROWS = 16
+NORM_PIECES = 8
 A_TILE = 1024
-B_TILE = 1536
+B_TILE = 768
 A_COLS = 5120
 A_CHUNKS = 5
 A_PER = A_COLS // A_CHUNKS
+Z_PIECES = A_COLS // TILE
 B_COLS = (WIDTH - A_COLS) // 2
 NEG = -1e30
 MESH = pl.DeviceIdType.MESH
@@ -280,16 +281,16 @@
         r = jnp.dot(vt[span], p_sc[slot], preferred_element_type=f32)[: HD + 8]
         acc[place, tile] = acc[place, tile] * a_sc[slot] + r
 
-    def opening(place, span, own=False):
+    def opening(place, span, own=False, base=0):
         s = scores_of(place, 0, span)
         if own:
             s = masked(place, 0, s)
-        s_sc[0] = s
-        t_sc[0] = fold(s)
-
-    def units(place, span_at, i, own=False, first=False, last=False):
+        s_sc[base] = s
+        t_sc[base] = fold(s)
+
+    def units(place, span_at, i, own=False, first=False, last=False, base=0):
         for tile in range(4):
-            cur, nxt = tile % 2, (tile + 1) % 2
+            cur, nxt = base + tile % 2, base + (tile + 1) % 2
             after, ai = (tile + 1) % 4, i + (tile + 1) // 4
             before, bi = (tile + 3) % 4, i - (1 if tile == 0 else 0)
             ends = last and tile == 3
@@ -321,15 +322,15 @@
             if not ends:
                 t_sc[nxt] = tops
 
-    def attend_own(place):
+    def attend_own(place, base=0):
         prepare(place)
         for tile in range(4):
             m_sc[place, tile] = jnp.full((1, 256), NEG, f32)
             acc[place, tile] = jnp.zeros((HD + 8, 256), f32)
-        opening(place, own_span(0, 0), True)
-        units(place, own_span, 0, own=True, first=True)
-        units(place, own_span, 1, last=True)
-        product(place, 3, own_span(3, 1), 1)
+        opening(place, own_span(0, 0), True, base)
+        units(place, own_span, 0, own=True, first=True, base=base)
+        units(place, own_span, 1, last=True, base=base)
+        product(place, 3, own_span(3, 1), base + 1)
 
     def attend_arriving():
         ready(0)
@@ -341,10 +342,11 @@
             src = posall.at[(ctx + 8 - i) % 8]
             rcopy(src, src, ps.at[0], pr.at[i - 1], mate).wait_recv()
         gathered(2)
-        attend_own(3)
         ready(1)
         opening(0, arriving_span(0, 2))
         for n in range(1, 8):
+            if n == 2:
+                attend_own(3, 2)
             if n in (2, 3, 5):
                 gathered({2: 4, 3: 5, 5: 7}[n])
             if n < 7:
@@ -397,8 +399,9 @@
                 for way in range(2):
                     arrived(recv.at[way, step - 1, :, piece], xr.at[way, step - 1, chunk])
 
-            for t in range(A_PER // A_TILE):
-                cols = pl.ds(chunk * A_PER + t * A_TILE, A_TILE)
+            tile = A_TILE if step < 3 else TILE
+            for t in range(A_PER // tile):
+                cols = pl.ds(chunk * A_PER + t * tile, tile)
                 r = projected(place, cols)
                 up, down = r[:ROWS], r[ROWS:]
                 if step > 0:
@@ -410,6 +413,8 @@
                 else:
                     summed[:, cols] = jnp.where(mine, up, down)
                     fin[:, cols] = jnp.where(mine, down, up).astype(bf16)
+                    n = chunk * (A_PER // TILE) + t
+                    start(rcopy(fin.at[:, cols], zrecv.at[:, cols], zs.at[n], zr.at[n], zmate))
 
             if step < 3:
                 for way, dev in ((0, xup), (1, xdn)):
@@ -419,15 +424,16 @@
                             xs.at[way, step, chunk], xr.at[way, step, chunk], dev,
                         )
                     )
-            else:
-                start(rcopy(fin.at[:, piece], zrecv.at[:, piece], zs.at[chunk], zr.at[chunk], zmate))
 
     def begin(ring, step, place):
         weights_here(*((5, 6) if ring == 0 else (6, 7)))
 
-        for t in range(B_COLS // B_TILE):
-            cols = pl.ds(t * B_TILE, B_TILE)
-            r = projected(place, pl.ds(A_COLS + ring * B_COLS + t * B_TILE, B_TILE))
+        @pl.loop(0, B_COLS // B_TILE)
+        def _(t):
+            cols = pl.ds(pl.multiple_of(t * B_TILE, B_TILE), B_TILE)
+            r = projected(
+                place, pl.ds(pl.multiple_of(A_COLS + ring * B_COLS + t * B_TILE, 256), B_TILE)
+            )
             bown[ring, step, :, cols] = jnp.where(mine, r[:ROWS], r[ROWS:])
             zsend[ring, step, :, cols] = jnp.where(mine, r[ROWS:], r[:ROWS]).astype(bf16)
 
@@ -482,8 +488,9 @@
     finish(0, 1)
 
     def meanwhile():
-        across(2, 2, range(3))
+        across(2, 2, range(1))
         finish(1, 0)
+        across(2, 2, range(1, 3))
 
     attend_others(3, meanwhile)
     begin(0, 3, 3)
@@ -512,30 +519,55 @@
         copy.start()
         stores.append(copy)
 
-    hand_out(A_CHUNKS, A_COLS, WIDTH, False)
-    for chunk in range(A_CHUNKS):
-        arrived(zrecv.at[:, pl.ds(chunk * A_PER, A_PER)], zr.at[chunk])
-        hand_out(chunk, chunk * A_PER, (chunk + 1) * A_PER, True)
+    hand_out(Z_PIECES, A_COLS, WIDTH, False)
+    for n in range(Z_PIECES):
+        arrived(zrecv.at[:, pl.ds(n * TILE, TILE)], zr.at[n])
+        hand_out(n, n * TILE, (n + 1) * TILE, True)
     for copy in stores:
         copy.wait()
     for copy in started:
         copy.wait_send()
 
 
-def norm_kernel(scale_ref, total_ref, gain_ref, hidden_ref, clipped_ref):
-    squares = jnp.zeros((NORM_ROWS, TILE), f32)
-    for t in range(0, WIDTH, TILE):
-        total = total_ref[:, t : t + TILE]
-        hidden_ref[:, t : t + TILE] = total.astype(bf16)
-        squares += total * total
+def norm_kernel(
+    scale_ref, total_hbm, gain_ref, hidden_hbm, clipped_hbm, total_ref, hidden_ref, clipped_ref, in_sem, h_sem, c_sem
+):
+    per = WIDTH // NORM_PIECES
+
+    def piece(n):
+        return pl.ds(n * per, per)
+
+    reads = [
+        pltpu.make_async_copy(total_hbm.at[:, piece(n)], total_ref.at[:, piece(n)], in_sem.at[n])
+        for n in range(NORM_PIECES)
+    ]
+    writes = []
+
+    def write(source, target, sem, n):
+        copy = pltpu.make_async_copy(source.at[:, piece(n)], target.at[:, piece(n)], sem.at[n])
+        copy.start()
+        writes.append(copy)
+
+    for copy in reads:
+        copy.start()
+    squares = jnp.zeros((ROWS, 128), f32)
+    for n in range(NORM_PIECES):
+        reads[n].wait()
+        for t in range(n * per, (n + 1) * per, 128):
+            total = total_ref[:, t : t + 128]
+            hidden_ref[:, t : t + 128] = total.astype(bf16)
+            squares += total * total
+        write(hidden_ref, hidden_hbm, h_sem, n)
     inv_rms = lax.rsqrt(jnp.sum(squares, axis=1, keepdims=True) * (1.0 / WIDTH) + 1e-5)
+    inv_rms = jnp.broadcast_to(inv_rms, (ROWS, 128))
     limit = 448.0 * scale_ref[0]
-    per = TILE // 128
-    for t in range(WIDTH // TILE):
-        cols = slice(t * TILE, (t + 1) * TILE)
-        gain = jnp.concatenate([gain_ref[t * per + i : t * per + i + 1, :] for i in range(per)], axis=1)
-        value = total_ref[:, cols] * inv_rms * gain
-        clipped_ref[:, cols] = jnp.minimum(jnp.maximum(value, -limit), limit).astype(bf16)
+    for n in range(NORM_PIECES):
+        for t in range(n * per, (n + 1) * per, 128):
+            value = total_ref[:, t : t + 128] * inv_rms * gain_ref[t // 128 : t // 128 + 1, :]
+            clipped_ref[:, t : t + 128] = jnp.minimum(jnp.maximum(value, -limit), limit).astype(bf16)
+        write(clipped_ref, clipped_hbm, c_sem, n)
+    for copy in writes:
+        copy.wait()
 
 
 def shards(queries, context_keys, context_values, positions, out_weight, residual_in, norm_gain, static_scale):
@@ -556,10 +588,10 @@
             pltpu.VMEM((4, 4, 2 * HD, 256), bf16),
             pltpu.VMEM((4, 4, HD + 8, 256), f32),
             pltpu.VMEM((4, 4, 1, 256), f32),
-            pltpu.VMEM((2, 1, 256), f32),
-            pltpu.VMEM((2, 8, 256), f32),
-            pltpu.VMEM((2, SPAN, 256), f32),
-            pltpu.VMEM((2, SPAN, 256), bf16),
+            pltpu.VMEM((4, 1, 256), f32),
+            pltpu.VMEM((4, 8, 256), f32),
+            pltpu.VMEM((4, SPAN, 256), f32),
+            pltpu.VMEM((4, SPAN, 256), bf16),
             pltpu.VMEM((4, 2 * ROWS, 1024), bf16),
             pltpu.VMEM((2, 3, ROWS, A_COLS), bf16),
             pltpu.VMEM((2, 3, ROWS, A_COLS), bf16),
@@ -572,9 +604,9 @@
             pltpu.VMEM((ROWS, A_COLS), bf16),
             pltpu.VMEM((ROWS, WIDTH), f32),
             pltpu.VMEM((ROWS, WIDTH), bf16),
-            dma((8,)), dma((A_CHUNKS + 1,)), dma((2,)), dma((2, 8)), dma((12,)), dma((12,)), dma((12,)), dma((12,)), dma((7,)), dma((7,)),
+            dma((8,)), dma((Z_PIECES + 1,)), dma((2,)), dma((2, 8)), dma((12,)), dma((12,)), dma((12,)), dma((12,)), dma((7,)), dma((7,)),
             dma((2, 3, A_CHUNKS)), dma((2, 3, A_CHUNKS)), dma((2, 4)), dma((2, 4)), dma((2, 3)), dma((2, 3)),
-            dma((A_CHUNKS,)), dma((A_CHUNKS,)),
+            dma((Z_PIECES,)), dma((Z_PIECES,)),
         ],
         compiler_params=pltpu.CompilerParams(
             collective_id=0, has_side_effects=True, vmem_limit_bytes=62 * 1024 * 1024
@@ -588,17 +620,17 @@
         residual_in,
     )
     out = jax.ShapeDtypeStruct((ROWS, WIDTH), bf16)
-    rows = pl.BlockSpec((NORM_ROWS, WIDTH), lambda i: (i, 0))
     return pl.pallas_call(
         norm_kernel,
-        grid=(ROWS // NORM_ROWS,),
         out_shape=(out, out),
-        in_specs=[
-            pl.BlockSpec(memory_space=pltpu.SMEM),
-            rows,
-            pl.BlockSpec((WIDTH // 128, 128), lambda i: (0, 0)),
+        in_specs=[pl.BlockSpec(memory_space=pltpu.SMEM), anywhere, pl.BlockSpec(memory_space=pltpu.VMEM)],
+        out_specs=(anywhere, anywhere),
+        scratch_shapes=[
+            pltpu.VMEM((ROWS, WIDTH), f32),
+            pltpu.VMEM((ROWS, WIDTH), bf16),
+            pltpu.VMEM((ROWS, WIDTH), bf16),
+            dma((NORM_PIECES,)), dma((NORM_PIECES,)), dma((NORM_PIECES,)),
         ],
-        out_specs=(rows, rows),
     )(static_scale, total, norm_gain.reshape(WIDTH // 128, 128))
 
 

time: 103 us -> 102 us (level)
  no operation moved by 1% of the time
where the time goes in v4:
time: 102 us
  Pallas kernels  101 us (99%)
  between operations  1.47 us (1%)
    pallas_call x1, Pallas kernels, shards(): pl.pallas_call(kernel, out_shape=jax.ShapeDtypeStruct((ROWS, WIDTH), f32)...  96.9 us
    pallas_call x1, Pallas kernels, shards(): pl.pallas_call(norm_kernel, out_shape=(out, out), in_specs=[pl.BlockSpec(...  3.64 us

profile of v4, /device:TPU:1, one launch (start us, length us, event | category | flops | bytes accessed | tf_op | source)
XLA Modules:
  0.0 102.0 jit_solution(17568251187963821149)
XLA Ops:
  1.3 96.9 %shard_map.95.total_hbm = f32[64,8192]{1,0:T(8,128)} custom-call(bf16[8,2,64,512]{3,2,1,0:T(8,128)(2,1)} %bitcast.7, bf16[2,512,1024]{2,1,0:T(8,128)(2,1)} %bitcast.5, bf16[2,512,1024]{2,1,0:T(8,128)(2,1)} %bitcast.6, s32[8,128]{1,0:T(8,128)} %bitcast.9, bf16[512,8192]{1,0:T(8,128)(2,1)} %w_hbm.1, bf16[64,8192]{1,0:T(8,128)(2,1)} %res_hbm.1), custom_call_target="tpu_custom_call" | custom-call | tf_op jit(solution)/shard_map/pallas_call | solution.py:576
  98.2 3.6 %shard_map.96 = (bf16[64,8192]{1,0:T(8,128)(2,1)}, bf16[64,8192]{1,0:T(8,128)(2,1)}) custom-call(f32[1]{0:T(128)S(6)} %copy.10.scale_ref, f32[64,8192]{1,0:T(8,128)} %shard_map.95.total_hbm, f32[64,128]{1,0:T(8,128)} %bitcast.8), custom_call_target="tpu_custom_call" | custom-call | tf_op jit(solution)/shard_map/pallas_call | solution.py:623
